TPU v7x, 32 devices: a whole 2x2x4 slice. The times are simulated.
32 devices in a mesh: grp: 2 (over y), brick: 4 (over z), vec: 2 (over x), sub: 2 (over core).
Axes of the slice: x: 2, y: 2, z: 4, core: 2. Of those that a mesh axis runs over, the one named last changes fastest.
Arguments:
- vectors: float32 [128, 3, 2, 16384], P(('vec', 'sub'), None, None, ('grp', 'brick')), parts along dimension 3, may hold values from -6 to 6
- gauge_links: float32 [3, 3, 3, 2, 16384], P(None, None, None, None, ('grp', 'brick')), parts along dimension 4, may hold values from -1 to 1, as said below
- momenta: int32 [27, 3], replicated, may hold values from -3 to 3
Outputs:
- elementals: float32 [128, 54, 2, 128], P(('vec', 'sub'), 'grp', None, 'brick'), parts along dimension 1
There are 2 independent parts, one for each index of `grp`. A program takes and returns all parts, laid end to end along the dimension named above; an argument that names none is the same for every part. Nothing has to cross between parts.
Inputs may be any that keep to these rules, and one draw needn't show every extreme that they name: Each gauge_links[mu, :, :, :, s] is a unitary 3x3 complex matrix.
All inputs are finite; a program needn't handle non-finite values.
Results may differ from a plain program's by a relative error of at most 0.0049.
Values may be sent and summed in bfloat16 or wider, within the bound.
A program may use at most 128 MiB of HBM per device.

v0:
```python
import math

import jax
import jax.numpy as jnp
from jax import lax
from jax.sharding import PartitionSpec as P

LY = 64
LZ = 8
ITERS = 2


KAPPA = 0.125


def from_behind(array, axis, by):
    peers = lax.axis_size(axis)
    return lax.ppermute(array, axis, [(i, (i + by) % peers) for i in range(peers)])


def padded_2(array, sides, width):
    for axis, dim in sides:
        peers, length = (lax.axis_size(axis), array.shape[dim])
        up = [(i, (i + 1) % peers) for i in range(peers)]
        down = [(j, i) for i, j in up]
        last = lax.slice_in_dim(array, length - width, length, axis=dim)
        initial = lax.slice_in_dim(array, 0, width, axis=dim)
        before = lax.ppermute(last, axis, up)
        after = lax.ppermute(initial, axis, down)
        array = jnp.concatenate([before, array, after], axis=dim)
    return array


def matrix_apply(matrix, source):
    matrix_real = matrix[:, :, 0][None]
    matrix_imag = matrix[:, :, 1][None]
    source_real = source[:, None, :, 0]
    source_imag = source[:, None, :, 1]
    real_part = jnp.sum(matrix_real * source_real - matrix_imag * source_imag, axis=2)
    imag_part = jnp.sum(matrix_real * source_imag + matrix_imag * source_real, axis=2)
    return jnp.stack([real_part, imag_part], axis=2)


def adjoint(matrix):
    return jnp.stack(
        [jnp.swapaxes(matrix[:, :, 0], 0, 1), -jnp.swapaxes(matrix[:, :, 1], 0, 1)], axis=2
    )


def step_depth(values, offset):
    depth_index = lax.iota(jnp.int32, values.shape[-1]) % LZ
    if offset > 0:
        return jnp.where(
            depth_index == LZ - 1, jnp.roll(values, LZ - 1, -1), jnp.roll(values, -1, -1)
        )
    return jnp.where(depth_index == 0, jnp.roll(values, 1 - LZ, -1), jnp.roll(values, 1, -1))


def step_column(values, offset):
    plane = LY * LZ
    column_index = lax.iota(jnp.int32, values.shape[-1]) // LZ % LY
    if offset > 0:
        return jnp.where(
            column_index == LY - 1, jnp.roll(values, plane - LZ, -1), jnp.roll(values, -LZ, -1)
        )
    return jnp.where(column_index == 0, jnp.roll(values, LZ - plane, -1), jnp.roll(values, LZ, -1))


def laplace_step(center, ahead, behind, here_links, back_links):
    forward = matrix_apply(here_links[0], ahead)
    backward = matrix_apply(adjoint(back_links), behind)
    total = forward + backward
    for direction, stepper in ((1, step_column), (2, step_depth)):
        forward = matrix_apply(here_links[direction], stepper(center, 1))
        backward = matrix_apply(adjoint(stepper(here_links[direction], -1)), stepper(center, -1))
        total = total + (forward + backward)
    return center + KAPPA * (total - 6.0 * center)


def shards(vectors, gauge_links, momenta):
    plane = LY * LZ
    local_sites = vectors.shape[3]
    raw_low = vectors.astype(jnp.bfloat16)
    field = vectors
    x_links = gauge_links[0]
    rim = from_behind(x_links[..., local_sites - plane :], "brick", 1)
    back_links = jnp.concatenate([rim, x_links[..., : local_sites - plane]], axis=3)
    for step in range(ITERS):
        padded = padded_2(field, (("brick", 3),), plane)
        field = laplace_step(
            padded[..., plane : plane + local_sites],
            padded[..., 2 * plane :],
            padded[..., :local_sites],
            gauge_links,
            back_links,
        )
    smeared_low = field.astype(jnp.bfloat16)
    raw_sites, smeared_sites = (
        lax.all_to_all(raw_low, ("vec", "sub"), split_axis=3, concat_axis=0, tiled=True),
        lax.all_to_all(smeared_low, ("vec", "sub"), split_axis=3, concat_axis=0, tiled=True),
    )
    groups = lax.axis_size(("vec", "sub"))
    total_vec = raw_sites.shape[0]
    width = raw_sites.shape[3]
    total_x = lax.axis_size("brick") * (local_sites // plane)
    first_site = lax.axis_index("brick") * local_sites + lax.axis_index(("vec", "sub")) * width
    site = first_site + lax.iota(jnp.int32, width)
    layer_index = (site // plane)[None]
    column_index = (site // LZ % LY)[None]
    depth_index = (site % LZ)[None]
    fraction = (
        jnp.mod(momenta[:, 0:1] * layer_index, total_x).astype(jnp.float32) / total_x
        + jnp.mod(momenta[:, 1:2] * column_index, LY).astype(jnp.float32) / LY
        + jnp.mod(momenta[:, 2:3] * depth_index, LZ).astype(jnp.float32) / LZ
    )
    angle = 2.0 * math.pi * fraction
    cosines = jnp.cos(angle)
    sines = jnp.sin(angle)
    right = smeared_sites.reshape((total_vec, 6 * width))
    scale = (3.0 * total_x * plane) ** (-0.5)

    def one_momentum(angles):
        cosine, sine = angles
        real_part = raw_sites[:, :, 0] * cosine - raw_sites[:, :, 1] * sine
        imag_part = raw_sites[:, :, 0] * sine + raw_sites[:, :, 1] * cosine
        phased = jnp.stack([real_part, imag_part], axis=2).astype(jnp.bfloat16)
        turned = jnp.stack([-phased[:, :, 1], phased[:, :, 0]], axis=2)
        left = jnp.concatenate(
            [
                phased.reshape((lax.axis_size(("vec", "sub")) * (total_vec // groups), 6 * width)),
                turned.reshape((lax.axis_size(("vec", "sub")) * (total_vec // groups), 6 * width)),
            ],
            axis=0,
        )
        product = lax.dot_general(
            left, right, (((1,), (1,)), ((), ())), preferred_element_type=jnp.float32
        )
        return product.reshape(
            (2, lax.axis_size(("vec", "sub")) * (total_vec // groups), total_vec)
        )

    blocks = lax.map(one_momentum, (cosines, sines))
    shares = lax.psum_scatter(
        jnp.transpose(blocks, (2, 0, 1, 3)) * scale, ("vec", "sub"), scatter_dimension=0, tiled=True
    )
    return lax.psum_scatter(shares, "brick", scatter_dimension=3, tiled=True)


def solution(mesh):
    in_specs = (
        P(("vec", "sub"), None, None, ("grp", "brick")),
        P(None, None, None, None, ("grp", "brick")),
        P(),
    )
    out_specs = P(("vec", "sub"), "grp", None, "brick")
    return jax.shard_map(shards, mesh=mesh, in_specs=in_specs, out_specs=out_specs, check_vma=False)
```

profile of v0, /device:TPU:1, one launch (start us, length us, event | category | flops | bytes accessed | tf_op | source)
XLA Modules:
  0.0 436.7 jit_solution(8413157391000246804)
XLA Ops:
  8.2 2.1 collective-permute-start.1
  12.6 2.1 collective-permute-start
  16.4 5.7 %copy.252 = bf16[32,3,2,2048]{0,2,1,3:T(2,128)(2,1)} copy(bf16[32,3,2,2048]{3,0,2,1:T(8,128)(2,1)S(1)} %copy.339) | data formatting | bytes 1572864 | tf_op jit(solution)/shard_map/convert_element_type | solution.py:83
  22.1 5.4 %reshape.114 = bf16[4,2,49152]{2,1,0:T(2,128)(2,1)} reshape(bf16[2048,3,2,32]{3,2,1,0:T(2,128)(2,1)} %bitcast.170) | data formatting | bytes 1572864
  27.5 5.6 %all-to-all-start = ((bf16[4,2,49152]{2,1,0:T(2,128)(2,1)}), bf16[4,2,49152]{2,1,0:T(2,128)(2,1)}, u32[]{:S(2)}, u32[]{:S(2)}) async-start(bf16[4,2,49152]{2,1,0:T(2,128)(2,1)} %reshape.114), calls=%async_computation | async-start | bytes 1572864 | tf_op jit(solution)/shard_map/all_to_all | solution.py:99
  36.5 1.8 fusion.62
  38.3 1.8 fusion.65
  40.1 1.8 fusion.61
  53.3 1.8 subtract_reduce_fusion.9
  55.1 1.8 subtract_reduce_fusion.6
  56.9 1.8 subtract_reduce_fusion.7
  66.7 2.0 fusion.11
  72.6 2.4 collective-permute-start.3
  81.7 2.7 collective-permute-done.4
  84.4 6.9 %collective-permute-done.3 = f32[32,3,2,512]{3,0,2,1:T(8,128)S(1)} collective-permute-done((f32[32,3,2,512]{3,0,2,1:T(8,128)S(1)}, f32[32,3,2,512]{3,0,2,1:T(8,128)S(1)}, u32[]{:S(2)}, u32[]{:S(2)}) %collective-permute-start.3) | collective-permute-done | bytes 393248 | tf_op jit(solution)/shard_map/ppermute | solution.py:29
  92.9 3.8 fusion.17
  96.7 7.5 %copy.282 = bf16[32,3,2,2048]{0,2,1,3:T(2,128)(2,1)S(1)} copy(bf16[32,3,2,2048]{3,0,2,1:T(8,128)(2,1)} %fusion.17) | data formatting | bytes 1572864 | tf_op jit(solution)/shard_map/convert_element_type | solution.py:97
  104.2 3.8 reshape.116
  108.0 4.8 %all-to-all-start.1 = ((bf16[4,2,49152]{2,1,0:T(2,128)(2,1)}), bf16[4,2,49152]{2,1,0:T(2,128)(2,1)S(1)}, u32[]{:S(2)}, u32[]{:S(2)}) async-start(bf16[4,2,49152]{2,1,0:T(2,128)(2,1)} %reshape.116), calls=%async_computation.1 | async-start | bytes 1572864 | tf_op jit(solution)/shard_map/all_to_all | solution.py:100
  113.3 4.5 %reshape.115 = bf16[2048,3,2,32]{3,2,1,0:T(2,128)(2,1)} reshape(bf16[4,2,49152]{2,1,0:T(2,128)(2,1)} %all-to-all-done) | data formatting | bytes 1572864
  117.8 6.7 %copy.253 = bf16[4,32,3,2,512]{4,1,0,3,2:T(8,128)(2,1)S(1)} copy(bf16[4,32,3,2,512]{1,3,2,4,0:T(2,128)(2,1)} %bitcast.172) | data formatting | bytes 1572864 | tf_op jit(solution)/shard_map/all_to_all | solution.py:99
  124.6 2.9 reshape.117
  127.5 7.3 %copy.283 = bf16[4,32,3,2,512]{4,3,2,1,0:T(2,128)(2,1)S(1)} copy(bf16[4,32,3,2,512]{1,3,2,4,0:T(2,128)(2,1)} %bitcast.173) | data formatting | bytes 1572864 | tf_op jit(solution)/shard_map/all_to_all | solution.py:100
  136.3 98.4 %while.10 = (s32[]{:T(128)}, f32[27,2,128,128]{3,2,1,0:T(8,128)}, bf16[128,3,2,512]{3,0,2,1:T(8,128)(2,1)S(1)}, f32[27,512]{1,0:T(8,128)S(1)}, f32[27,512]{1,0:T...) while((s32[]{:T(128)}, f32[27,2,128,128]{3,2,1,0:T(8,128)}, bf16[128,3,2,512]{3,0,2,1:T(8,128)(2,1)S(1)}, ...), condition=%wide.region_25.26_spmd, body=%wide.region_24.25_spmd.sunk | while | flops 207421440 | bytes 12202077 | solution.py:142
  234.7 2.3 multiply_bitcast_fusion
  237.0 4.5 %copy.284 = f32[128,27,2,128]{3,2,1,0:T(2,128)} copy(f32[128,27,2,128]{3,0,2,1:T(8,128)S(1)} %multiply_bitcast_fusion) | data formatting | bytes 7077888 | tf_op jit(solution)/shard_map/mul | solution.py:144
  243.4 73.2 %all-reduce.3.cloned.1.call-done = f32[128,27,2,128]{3,2,1,0:T(2,128)} async-done(((f32[128,27,2,128]{3,2,1,0:T(2,128)}), f32[128,27,2,128]{3,2,1,0:T(2,128)}) %all-reduce.3.cloned.1.call-update) | async-done | bytes 3538960
  317.9 33.9 %copy.285 = f32[32,27,2,128]{2,1,0,3:T(8,128)} copy(f32[32,27,2,128]{3,2,1,0:T(2,128)S(1)} %constant_dynamic-slice_fusion.2) | data formatting | bytes 1769472
  351.8 31.7 %reshape.111 = f32[128,1728]{1,0:T(8,128)} reshape(f32[128,32,27,2]{3,2,1,0:T(8,128)} %bitcast.71) | data formatting | bytes 1769472
  383.5 25.1 %reduce-scatter.4.cloned.1.call-done = f32[32,1728]{1,0:T(8,128)} async-done(((f32[128,1728]{1,0:T(8,128)}), f32[32,1728]{1,0:T(8,128)}) %reduce-scatter.4.cloned.1.call-update) | async-done | bytes 221200
  408.7 8.8 %reshape.112 = f32[32,32,27,2]{3,2,1,0:T(8,128)} reshape(f32[32,1728]{1,0:T(8,128)} %reduce-scatter.4.cloned.1.call-done) | data formatting | bytes 442368
  417.4 11.9 %copy.286 = f32[32,27,2,32]{3,2,1,0:T(2,128)} copy(f32[32,27,2,32]{2,1,0,3:T(8,128)} %bitcast.166) | data formatting | bytes 442368
  (401 shorter events, 141.5 us)
Async XLA Ops:
  8.2 7.3 %copy-start = (f32[32,3,2,2048]{3,2,1,0:T(2,128)S(1)}, f32[32,3,2,2048]{3,2,1,0:T(2,128)}, u32[]{:S(2)}) copy-start(f32[32,3,2,2048]{3,2,1,0:T(2,128)} %param.5) | copy-start | bytes 4718596
  8.2 51.1 %collective-permute-start.1 = (f32[3,3,2,512]{3,2,1,0:T(2,128)}, f32[3,3,2,512]{3,2,1,0:T(2,128)S(1)}, u32[]{:S(2)}, u32[]{:S(2)}) collective-permute-start(f32[3,3,2,512]{3,2,1,0:T(2,128)} %slice.441), channel_id=1, source_target_pairs={{0,4},{4,8},{8,12},{12,0},{1,5},{5,9},{9,13},{13,1},{2,6},{6,10},{... | collective-permute-start | bytes 110600 | tf_op jit(solution)/shard_map/ppermute | solution.py:18
  12.6 50.1 %collective-permute-start = (f32[32,3,2,512]{3,0,2,1:T(8,128)}, f32[32,3,2,512]{3,0,2,1:T(8,128)}, u32[]{:S(2)}, u32[]{:S(2)}) collective-permute-start(f32[32,3,2,512]{3,0,2,1:T(8,128)} %copy.321), channel_id=1, source_target_pairs={{4,0},{8,4},{12,8},{0,12},{5,1},{9,5},{13,9},{1,13},{6,2},{10,6},{... | collective-permute-start | bytes 1179656 | tf_op jit(solution)/shard_map/ppermute | solution.py:29
  15.5 45.0 %collective-permute-start.2 = (f32[32,3,2,512]{3,0,2,1:T(8,128)}, f32[32,3,2,512]{3,0,2,1:T(8,128)}, u32[]{:S(2)}, u32[]{:S(2)}) collective-permute-start(f32[32,3,2,512]{3,0,2,1:T(8,128)} %copy.322), channel_id=1, source_target_pairs={{0,4},{4,8},{8,12},{12,0},{1,5},{5,9},{9,13},{13,1},{2,6},{6,10},{... | collective-permute-start | bytes 1179656 | tf_op jit(solution)/shard_map/ppermute | solution.py:28
  27.5 80.6 %all-to-all-start = ((bf16[4,2,49152]{2,1,0:T(2,128)(2,1)}), bf16[4,2,49152]{2,1,0:T(2,128)(2,1)}, u32[]{:S(2)}, u32[]{:S(2)}) async-start(bf16[4,2,49152]{2,1,0:T(2,128)(2,1)} %reshape.114), calls=%async_computation | async-start | bytes 1572864 | tf_op jit(solution)/shard_map/all_to_all | solution.py:99
  42.8 14.1 %copy-start.7 = (f32[3,3,1,2048]{3,1,2,0:T(4,128)}, f32[3,3,1,2048]{3,1,2,0:T(4,128)S(1)}, u32[]{:S(2)}) copy-start(f32[3,3,1,2048]{3,1,2,0:T(4,128)S(1)} %copy.343) | copy-start | bytes 221188
  42.9 14.0 %copy-start.9 = (f32[3,3,1,2048]{3,1,2,0:T(4,128)}, f32[3,3,1,2048]{3,1,2,0:T(4,128)S(1)}, u32[]{:S(2)}) copy-start(f32[3,3,1,2048]{3,1,2,0:T(4,128)S(1)} %copy.342) | copy-start | bytes 221188
  52.5 0.8 copy-start.13
  52.5 0.8 copy-start.15
  52.6 2.5 copy-start.17
  52.6 2.5 copy-start.19
  63.8 0.9 copy-start.11
  63.8 0.9 copy-start.12
  63.8 1.6 copy-start.5
  63.8 1.6 copy-start.6
  64.8 1.3 copy-start.1
  64.8 1.5 copy-start.2
  64.8 1.7 copy-start.3
  64.8 2.0 copy-start.4
  71.4 13.1 %collective-permute-start.4 = (f32[32,3,2,512]{3,0,2,1:T(8,128)S(1)}, f32[32,3,2,512]{3,0,2,1:T(8,128)S(1)}, u32[]{:S(2)}, u32[]{:S(2)}) collective-permute-start(f32[32,3,2,512]{3,0,2,1:T(8,128)S(1)} %get-tuple-element.114), channel_id=1, source_target_pairs={{0,4},{4,8},{8,12},{12,0},{1,5},{5,9},{9,13},{13,1},{2,6},{6,10},{... | collective-permute-start | bytes 1179656 | tf_op jit(solution)/shard_map/ppermute | solution.py:28
  72.6 18.8 %collective-permute-start.3 = (f32[32,3,2,512]{3,0,2,1:T(8,128)S(1)}, f32[32,3,2,512]{3,0,2,1:T(8,128)S(1)}, u32[]{:S(2)}, u32[]{:S(2)}) collective-permute-start(f32[32,3,2,512]{3,0,2,1:T(8,128)S(1)} %get-tuple-element.115), channel_id=1, source_target_pairs={{4,0},{8,4},{12,8},{0,12},{5,1},{9,5},{13,9},{1,13},{6,2},{10,6},{... | collective-permute-start | bytes 1179656 | tf_op jit(solution)/shard_map/ppermute | solution.py:29
  77.6 0.9 copy-start.18
  77.6 0.9 copy-start.20
  78.5 0.9 copy-start.8
  78.5 0.9 copy-start.10
  79.5 0.9 copy-start.14
  79.5 0.9 copy-start.16
  108.0 4.9 %copy-start.21 = (s32[27,3]{0,1:T(4,128)S(1)}, s32[27,3]{0,1:T(4,128)}, u32[]{:S(2)}) copy-start(s32[27,3]{0,1:T(4,128)} %param.7) | copy-start | bytes 976
  108.0 16.5 %all-to-all-start.1 = ((bf16[4,2,49152]{2,1,0:T(2,128)(2,1)}), bf16[4,2,49152]{2,1,0:T(2,128)(2,1)S(1)}, u32[]{:S(2)}, u32[]{:S(2)}) async-start(bf16[4,2,49152]{2,1,0:T(2,128)(2,1)} %reshape.116), calls=%async_computation.1 | async-start | bytes 1572864 | tf_op jit(solution)/shard_map/all_to_all | solution.py:100
  112.8 203.8 %all-reduce.3.cloned.1.call-start = ((), (), s32[]{:S(2)}) async-start(), calls=%async_computation.4 | async-start | bytes 7077888
  241.5 0.7 copy-start.22
  241.6 167.1 %reduce-scatter.4.cloned.1.call-start = ((), (), s32[]{:S(2)}) async-start(), calls=%async_computation.3 | async-start | bytes 1146880
Sparse Core Ops, SparseCore 0:
  241.7 74.9 all-reduce.2
  383.6 24.9 reduce-scatter.3
where the time goes:
time: 444 us; the launch traced here: 437 us
  local copies, waits for them, and re-layouts  208 us (47%)
  waiting for transfers between devices  108 us (24%)
  matrix products  47 us (11%)
  other arithmetic  38.3 us (9%)
  starting transfers between devices  18.4 us (4%)
  between operations  15.3 us (3%)
    unnamed x81, local copies, waits for them, and re-layouts  119 us
    unnamed x4, waiting for transfers between devices  98.4 us
    dot_general x27, matrix products, one_momentum(): lax.dot_general(left, right, (((1,), (1,)), ((), ())), preferred_element_...  47 us
    dynamic_update_slice x27, local copies, waits for them, and re-layouts, shards(): blocks = lax.map(one_momentum, (cosines, sines))  17.9 us
    reduce_sum x12, other arithmetic, matrix_apply(): jnp.sum(matrix_real * source_real - matrix_imag * source_imag, axis=2)  11.3 us
    convert_element_type x27, local copies, waits for them, and re-layouts, one_momentum(): phased = jnp.stack([real_part, imag_part], axis=2).astype(jnp.bfloat16)  9.99 us
    another operation x27, local copies, waits for them, and re-layouts, one_momentum(): turned = jnp.stack([-phased[:, :, 1], phased[:, :, 0]], axis=2)  9.99 us
  transfers between devices with their start and end apart: 9, of which 4 were waited for; matrix products, arithmetic and copies ran while one was open for 20% of the time, Pallas kernels for 0%

commit v1 on v0

--- a/solution.py
+++ b/solution.py
@@ -1,8 +1,11 @@
+import functools
 import math
 
 import jax
 import jax.numpy as jnp
 from jax import lax
+from jax.experimental import pallas as pl
+from jax.experimental.pallas import tpu as pltpu
 from jax.sharding import PartitionSpec as P
 
 LY = 64
@@ -146,6 +149,258 @@
     return lax.psum_scatter(shares, "brick", scatter_dimension=3, tiled=True)
 
 
+def smear_kernel(planes, rows, x_ref, lo_ref, hi_ref, lk_ref, lb_ref, la_ref, out_ref, stage, table, f0, f1, moved):
+    plane = LY * LZ
+    f32 = jnp.float32
+    blocks = rows // 8
+    depth = lax.broadcasted_iota(jnp.int32, (8, plane), 1) % LZ
+    link_depth = lax.broadcasted_iota(jnp.int32, (56, plane), 1) % LZ
+
+    for k in range(6):
+        f0[k] = lo_ref[k].astype(f32)
+        f0[6 + 3 * planes + k] = hi_ref[k].astype(f32)
+
+    def take(k, carry):
+        f0[6 + k] = x_ref[k]
+        return carry
+
+    lax.fori_loop(0, 3 * planes, take, 0)
+    for k in range(2):
+        stage[k, 0:54] = lb_ref[k].astype(f32)
+    for k in range(planes):
+        stage[2 + k, 0:54] = lk_ref[k]
+    stage[2 + planes, 0:54] = la_ref[0].astype(f32)
+
+    def spread(t, carry):
+        here = stage[t + 1]
+        behind_x = stage[t]
+        behind_y = pltpu.roll(here, LZ, 1)
+        behind_z = jnp.where(
+            link_depth == 0, pltpu.roll(here, plane - (LZ - 1), 1), pltpu.roll(here, 1, 1)
+        )
+        for r in range(54):
+            table[t, r] = jnp.broadcast_to(here[r : r + 1], (8, plane))
+            back = (behind_x, behind_y, behind_z)[r // 18]
+            table[t, 54 + r] = jnp.broadcast_to(back[r : r + 1], (8, plane))
+        return carry
+
+    lax.fori_loop(0, planes + 2, spread, 0)
+
+    def one_plane(source, at, links, target, to):
+        def shift(k, carry):
+            c, b = k // blocks, k % blocks
+            rows_at = pl.ds(pl.multiple_of(b * 8, 8), 8)
+            for half in range(2):
+                lanes = slice(half * plane, (half + 1) * plane)
+                v = source[at * 3 + c, rows_at, lanes]
+                moved[0, c, rows_at, lanes] = pltpu.roll(v, plane - LZ, 1)
+                moved[1, c, rows_at, lanes] = pltpu.roll(v, LZ, 1)
+                moved[2, c, rows_at, lanes] = jnp.where(
+                    depth == LZ - 1, pltpu.roll(v, LZ - 1, 1), pltpu.roll(v, plane - 1, 1)
+                )
+                moved[3, c, rows_at, lanes] = jnp.where(
+                    depth == 0, pltpu.roll(v, plane - (LZ - 1), 1), pltpu.roll(v, 1, 1)
+                )
+            return carry
+
+        lax.fori_loop(0, 3 * blocks, shift, 0)
+
+        def block(k, carry):
+            b, lane = k % blocks, k // blocks
+            rows_at = pl.ds(pl.multiple_of(b * 8, 8), 8)
+            real_at = pl.ds(pl.multiple_of(lane * 128, 128), 128)
+            imag_at = pl.ds(pl.multiple_of(plane + lane * 128, 128), 128)
+            acc = [[None, None] for _ in range(3)]
+
+            def add(r, part, value):
+                acc[r][part] = value if acc[r][part] is None else acc[r][part] + value
+
+            for way in range(6):
+                direction, back = way // 2, way % 2
+                for c in range(3):
+                    if direction == 0:
+                        index = (at + 1 - 2 * back) * 3 + c
+                        sr = source[index, rows_at, real_at]
+                        si = source[index, rows_at, imag_at]
+                    else:
+                        sr = moved[way - 2, c, rows_at, real_at]
+                        si = moved[way - 2, c, rows_at, imag_at]
+                    for r in range(3):
+                        row = direction * 18 + (54 + c * 6 + r * 2 if back else r * 6 + c * 2)
+                        ur = table[links, row, :, real_at]
+                        ui = table[links, row + 1, :, real_at]
+                        if back:
+                            add(r, 0, ur * sr + ui * si)
+                            add(r, 1, ur * si - ui * sr)
+                        else:
+                            add(r, 0, ur * sr - ui * si)
+                            add(r, 1, ur * si + ui * sr)
+            for r in range(3):
+                for part, lanes in ((0, real_at), (1, imag_at)):
+                    mid = source[at * 3 + r, rows_at, lanes]
+                    target[to * 3 + r, rows_at, lanes] = mid + KAPPA * (acc[r][part] - 6.0 * mid)
+            return carry
+
+        lax.fori_loop(0, blocks * (plane // 128), block, 0)
+
+    def first(t, carry):
+        one_plane(f0, t + 1, t, f1, t)
+        return carry
+
+    lax.fori_loop(0, planes + 2, first, 0)
+
+    def second(t, carry):
+        one_plane(f1, t + 1, t + 1, f0, t)
+        return carry
+
+    lax.fori_loop(0, planes, second, 0)
+
+    def put(k, carry):
+        out_ref[k] = f0[k].astype(out_ref.dtype)
+        return carry
+
+    lax.fori_loop(0, 3 * planes, put, 0)
+
+
+def product_kernel(groups, rows, count, scale, order_ref, cos_ref, sin_ref, smeared_ref, *rest):
+    plane = LY * LZ
+    raw_refs = rest[:groups]
+    out_refs = rest[groups : 2 * groups]
+    right, left, wide, total = rest[2 * groups :]
+    total[...] = jnp.zeros_like(total)
+
+    def chunk(k, carry):
+        for u in range(groups):
+            raw = raw_refs[u][k]
+            first = 2 * rows * u
+            right[first : first + rows, :] = raw
+            right[first + rows : first + 2 * rows, 0:plane] = -raw[:, plane:]
+            right[first + rows : first + 2 * rows, plane:] = raw[:, :plane]
+        wide[...] = smeared_ref[k].astype(jnp.float32)
+
+        def turn(q, carry):
+            cosine = cos_ref[k // 3, pl.ds(q, 1), :]
+            sine = sin_ref[k // 3, pl.ds(q, 1), :]
+            sr = wide[:, 0:plane]
+            si = wide[:, plane:]
+            at = pl.ds(pl.multiple_of(q * rows, rows), rows)
+            left[at, 0:plane] = (cosine * sr + sine * si).astype(left.dtype)
+            left[at, plane:] = (cosine * si - sine * sr).astype(left.dtype)
+            return carry
+
+        lax.fori_loop(0, count, turn, 0)
+        total[...] += lax.dot_general(
+            right[...], left[...], (((1,), (1,)), ((), ())), preferred_element_type=jnp.float32
+        )
+        return carry
+
+    lax.fori_loop(0, smeared_ref.shape[0], chunk, 0)
+    for k in range(groups):
+        first = pl.multiple_of(order_ref[k] * (2 * rows), 2 * rows)
+        out_refs[k][...] = (total[pl.ds(first, 2 * rows), :] * scale).astype(out_refs[k].dtype)
+
+
+def phase_tables(momenta, local_sites, total_x):
+    plane = LY * LZ
+    site = lax.axis_index("brick") * local_sites + lax.iota(jnp.int32, local_sites)
+    site = site.reshape((local_sites // plane, 1, plane))
+    fraction = (
+        jnp.mod(momenta[None, :, 0:1] * (site // plane), total_x).astype(jnp.float32) / total_x
+        + jnp.mod(momenta[None, :, 1:2] * (site // LZ % LY), LY).astype(jnp.float32) / LY
+        + jnp.mod(momenta[None, :, 2:3] * (site % LZ), LZ).astype(jnp.float32) / LZ
+    )
+    angle = 2.0 * math.pi * fraction
+    return jnp.cos(angle), jnp.sin(angle)
+
+
+def shards_kernels(vectors, gauge_links, momenta):
+    plane = LY * LZ
+    rows, local_sites = vectors.shape[0], vectors.shape[3]
+    planes = local_sites // plane
+    bricks, vecs, subs = (lax.axis_size(a) for a in ("brick", "vec", "sub"))
+    groups = vecs * subs
+    count = momenta.shape[0]
+    low = jnp.bfloat16
+    wide = jnp.transpose(vectors.reshape((rows, 3, 2, planes, plane)), (3, 1, 0, 2, 4))
+    wide = wide.reshape((planes * 3, rows, 2 * plane))
+    raw = wide.astype(low)
+    below = from_behind(raw[-6:], "brick", 1)
+    above = from_behind(raw[:6], "brick", -1)
+    links = jnp.transpose(gauge_links.reshape((54, planes, plane)), (1, 0, 2))
+    links_low = links.astype(low)
+    links_below = from_behind(links_low[-2:], "brick", 1)
+    links_above = from_behind(links_low[:1], "brick", -1)
+    gathered = []
+    for kv in range(vecs):
+        one = raw if kv == 0 else from_behind(raw, "vec", -kv)
+        for ks in range(subs):
+            gathered.append(one if ks == 0 else from_behind(one, "sub", -ks))
+    cosines, sines = phase_tables(momenta, local_sites, bricks * planes)
+
+    vmem = pl.BlockSpec(memory_space=pltpu.VMEM)
+    smeared = pl.pallas_call(
+        functools.partial(smear_kernel, planes, rows),
+        out_shape=jax.ShapeDtypeStruct((planes * 3, rows, 2 * plane), low),
+        in_specs=[vmem] * 6,
+        out_specs=vmem,
+        scratch_shapes=[
+            pltpu.VMEM((planes + 3, 56, plane), jnp.float32),
+            pltpu.VMEM((planes + 2, 108, 8, plane), jnp.float32),
+            pltpu.VMEM(((planes + 4) * 3, rows, 2 * plane), jnp.float32),
+            pltpu.VMEM(((planes + 2) * 3, rows, 2 * plane), jnp.float32),
+            pltpu.VMEM((4, 3, rows, 2 * plane), jnp.float32),
+        ],
+        compiler_params=pltpu.CompilerParams(vmem_limit_bytes=48 * 2**20),
+        cost_estimate=pl.CostEstimate(
+            flops=432 * 2 * (planes + 1) * plane * rows * 4, bytes_accessed=4 * 2**20, transcendentals=0
+        ),
+        name="smear",
+    )(wide, below, above, links, links_below, links_above)
+
+    me_vec, me_sub, me_brick = (lax.axis_index(a) for a in ("vec", "sub", "brick"))
+    owner = (me_brick + lax.iota(jnp.int32, groups)) % groups
+    order = (owner // subs - me_vec) % vecs * subs + (owner % subs - me_sub) % subs
+    scale = (3.0 * bricks * local_sites) ** (-0.5)
+    blocks = pl.pallas_call(
+        functools.partial(product_kernel, groups, rows, count, scale),
+        out_shape=[jax.ShapeDtypeStruct((2 * rows, count * rows), low)] * groups,
+        in_specs=[pl.BlockSpec(memory_space=pltpu.SMEM)] + [vmem] * (3 + groups),
+        out_specs=[vmem] * groups,
+        scratch_shapes=[
+            pltpu.VMEM((2 * rows * groups, 2 * plane), low),
+            pltpu.VMEM((count * rows, 2 * plane), low),
+            pltpu.VMEM((rows, 2 * plane), jnp.float32),
+            pltpu.VMEM((2 * rows * groups, count * rows), jnp.float32),
+        ],
+        compiler_params=pltpu.CompilerParams(vmem_limit_bytes=40 * 2**20),
+        cost_estimate=pl.CostEstimate(
+            flops=2 * 2 * rows * groups * count * rows * 6 * local_sites,
+            bytes_accessed=8 * 2**20,
+            transcendentals=0,
+        ),
+        name="product",
+    )(order, cosines, sines, smeared, *gathered)
+
+    total = None
+    for k in range(groups):
+        pairs = [
+            (b * groups + u, u * groups + (b + k) % groups)
+            for b in range(bricks)
+            for u in range(groups)
+        ]
+        got = lax.ppermute(blocks[k], ("brick", "vec", "sub"), pairs).astype(jnp.float32)
+        total = got if total is None else total + got
+    return jnp.transpose(total.reshape((2, rows, count, rows)), (1, 2, 0, 3))
+
+
+def choose(vectors, gauge_links, momenta):
+    groups = lax.axis_size(("vec", "sub"))
+    planes = vectors.shape[3] // (LY * LZ)
+    if groups == lax.axis_size("brick") and planes >= 2 and vectors.shape[0] % 16 == 0:
+        return shards_kernels(vectors, gauge_links, momenta)
+    return shards(vectors, gauge_links, momenta)
+
+
 def solution(mesh):
     in_specs = (
         P(("vec", "sub"), None, None, ("grp", "brick")),
@@ -153,4 +408,4 @@
         P(),
     )
     out_specs = P(("vec", "sub"), "grp", None, "brick")
-    return jax.shard_map(shards, mesh=mesh, in_specs=in_specs, out_specs=out_specs, check_vma=False)
+    return jax.shard_map(choose, mesh=mesh, in_specs=in_specs, out_specs=out_specs, check_vma=False)

time: 444 us -> 120 us (0.27); the launches traced: 437 us -> 120 us
  local copies, waits for them, and re-layouts: 208 us -> 13.5 us
  waiting for transfers between devices: 108 us -> 30.5 us
  Pallas kernels: 0 us -> 55.2 us
  matrix products: 47 us -> 0 us
  other arithmetic: 38.3 us -> 2.38 us
  between operations: 15.3 us -> 0.17 us
    unnamed x81 -> x8, local copies, waits for them, and re-layouts: 119 us -> 0.02 us
    unnamed x4 -> x0, waiting for transfers between devices: 98.4 us -> none
    pallas_call x0 -> x2, Pallas kernels: none -> 55.2 us  [the longest x1 34.3 us: shards_kernels(): pl.pallas_call(functools.partial(smear_kernel, planes, rows), out_shape=j...]
    dot_general x27 -> x0, matrix products: 47 us -> none  [one_momentum(): lax.dot_general(left, right, (((1,), (1,)), ((), ())), preferred_element_...]
    convert_element_type x29 -> x0, local copies, waits for them, and re-layouts: 23.2 us -> none  [the longest x27 9.99 us: one_momentum(): phased = jnp.stack([real_part, imag_part], axis=2).astype(jnp.bfloat16)]
    dynamic_update_slice x27 -> x0, local copies, waits for them, and re-layouts: 17.9 us -> none  [shards(): blocks = lax.map(one_momentum, (cosines, sines))]
    all_to_all x2 -> x0, local copies, waits for them, and re-layouts: 14.1 us -> none  [the longest x1 7.32 us: shards(): lax.all_to_all(smeared_low, ('vec', 'sub'), split_axis=3, concat_axis=0,...]
    ppermute x1 -> x7, waiting for transfers between devices: 0.01 us -> 13.7 us  [from_behind(): lax.ppermute(array, axis, [(i, (i + by) % peers) for i in range(peers)])]
  transfers between devices with their start and end apart: 9 -> 11, of which waited for: 4 -> 4; matrix products, arithmetic and copies ran while one was open for 20% -> 7% of each run, Pallas kernels for 0% -> 29%
where the time goes in v1:
time: 120 us
  Pallas kernels  55.2 us (46%)
  waiting for transfers between devices  30.5 us (25%)
  starting transfers between devices  18.3 us (15%)
  local copies, waits for them, and re-layouts  13.5 us (11%)
  other arithmetic  2.38 us (2%)
    pallas_call x1, Pallas kernels, shards_kernels(): pl.pallas_call(functools.partial(smear_kernel, planes, rows), out_shape=j...  34.3 us
    pallas_call x1, Pallas kernels, shards_kernels(): pl.pallas_call(functools.partial(product_kernel, groups, rows, count, sca...  20.9 us
    ppermute x4, waiting for transfers between devices, shards_kernels(): lax.ppermute(blocks[k], ('brick', 'vec', 'sub'), pairs).astype(jnp.float32)  16.9 us
    ppermute x7, waiting for transfers between devices, from_behind(): lax.ppermute(array, axis, [(i, (i + by) % peers) for i in range(peers)])  13.7 us
    ppermute x7, starting transfers between devices, from_behind(): lax.ppermute(array, axis, [(i, (i + by) % peers) for i in range(peers)])  10.6 us
    ppermute x4, starting transfers between devices, shards_kernels(): lax.ppermute(blocks[k], ('brick', 'vec', 'sub'), pairs).astype(jnp.float32)  7.68 us
    reshape x2, local copies, waits for them, and re-layouts, shards_kernels(): vectors.reshape((rows, 3, 2, planes, plane))  3.71 us
    reshape x3, local copies, waits for them, and re-layouts, shards_kernels(): links = jnp.transpose(gauge_links.reshape((54, planes, plane)), (1, 0, 2))  2.42 us
  transfers between devices with their start and end apart: 11, of which 4 were waited for; matrix products, arithmetic and copies ran while one was open for 7% of the time, Pallas kernels for 29%

profile of v1, /device:TPU:1, one launch (start us, length us, event | category | flops | bytes accessed | tf_op | source)
XLA Modules:
  0.0 120.0 jit_solution(15895491391498213151)
XLA Ops:
  0.0 2.9 %reshape.164 = f32[32,3,2,4,512]{4,3,2,1,0:T(4,128)S(1)} reshape(f32[32,3,2,2048]{3,2,1,0:T(2,128)} %param.3) | data formatting | bytes 3145728 | tf_op jit(solution)/shard_map/reshape | solution.py:324
  2.9 0.8 copy.13
  3.7 1.4 %reshape.165.x_ref = f32[12,32,1024]{2,1,0:T(8,128)S(1)} reshape(f32[4,3,32,2,512]{4,3,2,1,0:T(2,128)S(1)} %bitcast.17) | data formatting | bytes 3145728 | tf_op jit(solution)/shard_map/reshape | solution.py:325
  5.1 0.1 convert_element_type.30.rest_0_
  5.2 2.1 %collective-permute-start.5 = (bf16[12,32,1024]{2,1,0:T(8,128)(2,1)S(1)}, bf16[12,32,1024]{2,1,0:T(8,128)(2,1)}, u32[]{:S(2)}, u32[]{:S(2)}) collective-permute-start(bf16[12,32,1024]{2,1,0:T(8,128)(2,1)S(1)} %convert_element_type.30.rest_0_), channel_id=1, source_target_pairs={{0,2},{2,0},{1,3},{3,1},{4,6},{6,4},{5,7},{7,5},{8,10},{10,8},{9,1... | collective-permute-start | bytes 2359304 | tf_op jit(solution)/shard_map/ppermute | solution.py:21
  7.3 1.0 collective-permute-start.4
  8.3 0.5 reshape.166
  8.7 0.0 copy-start.1
  8.8 0.8 copy.15
  9.6 1.4 %slice.31 = bf16[1,54,512]{2,1,0:T(8,128)(2,1)} slice(bf16[4,54,512]{2,1,0:T(8,128)(2,1)} %bitcast.15), slice={[0:1], [0:54], [0:512]} | slice | bytes 110592 | tf_op jit(solution)/shard_map/slice | solution.py:332
  11.0 3.3 %collective-permute-start.3 = (bf16[1,54,512]{2,1,0:T(8,128)(2,1)}, bf16[1,54,512]{2,1,0:T(8,128)(2,1)S(1)}, u32[]{:S(2)}, u32[]{:S(2)}) collective-permute-start(bf16[1,54,512]{2,1,0:T(8,128)(2,1)} %slice.31), channel_id=1, source_target_pairs={{0,12},{4,0},{8,4},{12,8},{1,13},{5,1},{9,5},{13,9},{2,14},{6,2},{... | collective-permute-start | bytes 165896 | tf_op jit(solution)/shard_map/ppermute | solution.py:21
  14.3 1.0 fusion.24
  15.3 0.2 collective-permute-start.1
  15.5 1.3 %collective-permute-start = (bf16[6,32,1024]{2,1,0:T(8,128)(2,1)}, bf16[6,32,1024]{2,1,0:T(8,128)(2,1)}, u32[]{:S(2)}, u32[]{:S(2)}) collective-permute-start(bf16[6,32,1024]{2,1,0:T(8,128)(2,1)} %get-tuple-element.14), channel_id=1, source_target_pairs={{0,4},{4,8},{8,12},{12,0},{1,5},{5,9},{9,13},{13,1},{2,6},{6,10},{... | collective-permute-start | bytes 1179656 | tf_op jit(solution)/shard_map/ppermute | solution.py:21
  16.8 7.9 %collective-permute-done.5.rest_2_ = bf16[12,32,1024]{2,1,0:T(8,128)(2,1)} collective-permute-done((bf16[12,32,1024]{2,1,0:T(8,128)(2,1)S(1)}, bf16[12,32,1024]{2,1,0:T(8,128)(2,1)}, u32[]{:S(2)}, u32[]{:S(2)}) %collective-permute-start.5) | collective-permute-done | bytes 786464 | tf_op jit(solution)/shard_map/ppermute | solution.py:21
  24.7 1.3 %collective-permute-start.6 = (bf16[12,32,1024]{2,1,0:T(8,128)(2,1)}, bf16[12,32,1024]{2,1,0:T(8,128)(2,1)}, u32[]{:S(2)}, u32[]{:S(2)}) collective-permute-start(bf16[12,32,1024]{2,1,0:T(8,128)(2,1)} %collective-permute-done.5.rest_2_), channel_id=1, source_target_pairs={{0,1},{1,0},{2,3},{3,2},{4,5},{5,4},{6,7},{7,6},{8,9},{9,8},{10,11... | collective-permute-start | bytes 2359304 | tf_op jit(solution)/shard_map/ppermute | solution.py:21
  26.0 2.1 %fusion.12 = (f32[4,27,512]{2,1,0:T(8,128)S(1)}, f32[4,27,512]{2,1,0:T(8,128)}) fusion(s32[4,512]{1,0:T(4,128)S(1)} %get-tuple-element.20, s32[27]{0:T(128)S(1)} %get-tuple-element.18, s32[4,512]{1,0:T(4,128)S(1)} %get-tuple-element.21, s32[27]{0:T(128)S(1)} %get-tuple-element.19, s32[4,512]{1,0:T(4,128)S(1)} %add_select_fusion.6, s32[27]{0:T(128)S(1)} %get-tuple-element.17), kind=kLoop, calls=%fused_computation.30 | loop fusion | flops 2488320 | bytes 467268 | tf_op jit(solution)/shard_map/sin | solution.py:313
  28.1 1.2 copy.14
  29.3 1.6 %slice.30 = bf16[2,54,512]{2,1,0:T(8,128)(2,1)} slice(bf16[4,54,512]{2,1,0:T(8,128)(2,1)} %bitcast.15), slice={[2:4], [0:54], [0:512]} | slice | bytes 221184 | tf_op jit(solution)/shard_map/slice | solution.py:331
  30.9 1.5 %collective-permute-start.2 = (bf16[2,54,512]{2,1,0:T(8,128)(2,1)}, bf16[2,54,512]{2,1,0:T(8,128)(2,1)S(1)}, u32[]{:S(2)}, u32[]{:S(2)}) collective-permute-start(bf16[2,54,512]{2,1,0:T(8,128)(2,1)} %slice.30), channel_id=1, source_target_pairs={{0,4},{4,8},{8,12},{12,0},{1,5},{5,9},{9,13},{13,1},{2,6},{6,10},{... | collective-permute-start | bytes 331784 | tf_op jit(solution)/shard_map/ppermute | solution.py:21
  32.4 5.7 %collective-permute-done.2.lb_ref = bf16[2,54,512]{2,1,0:T(8,128)(2,1)S(1)} collective-permute-done((bf16[2,54,512]{2,1,0:T(8,128)(2,1)}, bf16[2,54,512]{2,1,0:T(8,128)(2,1)S(1)}, u32[]{:S(2)}, u32[]{:S(2)}) %collective-permute-start.2) | collective-permute-done | bytes 110624 | tf_op jit(solution)/shard_map/ppermute | solution.py:21
  38.2 34.3 %smear.1.smeared_ref = bf16[12,32,1024]{2,1,0:T(8,128)(2,1)S(1)} custom-call(f32[12,32,1024]{2,1,0:T(8,128)S(1)} %reshape.165.x_ref, bf16[6,32,1024]{2,1,0:T(8,128)(2,1)} %collective-permute-done.lo_ref, bf16[6,32,1024]{2,1,0:T(8,128)(2,1)S(1)} %collective-permute-done.1.hi_ref, f32[4,54,512]{2,1,0:T(8,128)S(1)} %bitcast.16, ...), custom_call_target="tpu_custom_call" | custom-call | flops 283115520 | bytes 4194304 | tf_op jit(solution)/shard_map/smear/pallas_call | solution.py:341
  72.5 20.9 %product.1 = (bf16[64,864]{1,0:T(8,128)(2,1)S(1)}, bf16[64,864]{1,0:T(8,128)(2,1)S(1)}, bf16[64,864]{1,0:T(8,128)(2,1)S(1)}, bf16[64,864]{1,0:T(8,128)(2,1)S(1)}) custom-call(s32[4]{0:T(128)S(1)} %fusion.17.order_ref, f32[4,27,512]{2,1,0:T(8,128)S(1)} %copy-done, f32[4,27,512]{2,1,0:T(8,128)S(1)} %get-tuple-element.15.sin_ref, ...), custom_call_target="tpu_custom_call" | custom-call | flops 5435817984 | bytes 8388608 | tf_op jit(solution)/shard_map/product/pallas_call | solution.py:364
  93.4 1.9 %collective-permute-start.7 = (bf16[64,864]{1,0:T(8,128)(2,1)S(1)}, bf16[64,864]{1,0:T(8,128)(2,1)S(1)}, u32[]{:S(2)}, u32[]{:S(2)}) collective-permute-start(bf16[64,864]{1,0:T(8,128)(2,1)S(1)} %get-tuple-element.9), channel_id=1, source_target_pairs={{0,0},{1,4},{2,8},{3,12},{4,1},{5,5},{6,9},{7,13},{8,2},{9,6},{10,... | collective-permute-start | bytes 331784 | tf_op jit(solution)/shard_map/ppermute | solution.py:391
  95.3 0.1 collective-permute-start.8
  95.4 1.7 %collective-permute-start.9 = (bf16[64,864]{1,0:T(8,128)(2,1)S(1)}, bf16[64,864]{1,0:T(8,128)(2,1)S(1)}, u32[]{:S(2)}, u32[]{:S(2)}) collective-permute-start(bf16[64,864]{1,0:T(8,128)(2,1)S(1)} %get-tuple-element.11), channel_id=1, source_target_pairs={{0,2},{1,6},{2,10},{3,14},{4,3},{5,7},{6,11},{7,15},{8,0},{9,4},{1... | collective-permute-start | bytes 331784 | tf_op jit(solution)/shard_map/ppermute | solution.py:391
  97.1 4.0 %collective-permute-start.10 = (bf16[64,864]{1,0:T(8,128)(2,1)S(1)}, bf16[64,864]{1,0:T(8,128)(2,1)S(1)}, u32[]{:S(2)}, u32[]{:S(2)}) collective-permute-start(bf16[64,864]{1,0:T(8,128)(2,1)S(1)} %get-tuple-element.12), channel_id=1, source_target_pairs={{0,3},{1,7},{2,11},{3,15},{4,0},{5,4},{6,8},{7,12},{8,1},{9,5},{10... | collective-permute-start | bytes 331784 | tf_op jit(solution)/shard_map/ppermute | solution.py:391
  101.1 6.4 %collective-permute-done.9 = bf16[64,864]{1,0:T(8,128)(2,1)S(1)} collective-permute-done((bf16[64,864]{1,0:T(8,128)(2,1)S(1)}, bf16[64,864]{1,0:T(8,128)(2,1)S(1)}, u32[]{:S(2)}, u32[]{:S(2)}) %collective-permute-start.9) | collective-permute-done | bytes 110624 | tf_op jit(solution)/shard_map/ppermute | solution.py:391
  107.5 10.4 %collective-permute-done.10 = bf16[64,864]{1,0:T(8,128)(2,1)S(1)} collective-permute-done((bf16[64,864]{1,0:T(8,128)(2,1)S(1)}, bf16[64,864]{1,0:T(8,128)(2,1)S(1)}, u32[]{:S(2)}, u32[]{:S(2)}) %collective-permute-start.10) | collective-permute-done | bytes 110624 | tf_op jit(solution)/shard_map/ppermute | solution.py:391
  118.0 0.1 convert_add_fusion
  118.0 0.4 reshape.167
  118.4 1.6 %copy.8 = f32[32,27,2,32]{3,2,1,0:T(2,128)} copy(f32[32,27,2,32]{3,1,0,2:T(8,128)S(1)} %bitcast.18) | data formatting | bytes 442368 | tf_op jit(solution)/shard_map/transpose | solution.py:393
  (18 shorter events, 0.1 us)
Async XLA Ops:
  5.1 3.2 %copy-start.2 = (f32[3,3,3,2,2048]{4,3,2,1,0:T(2,128)S(1)}, f32[3,3,3,2,2048]{4,3,2,1,0:T(2,128)}, u32[]{:S(2)}) copy-start(f32[3,3,3,2,2048]{4,3,2,1,0:T(2,128)} %param.4) | copy-start | bytes 1327108
  5.2 20.7 %copy-start.3 = (s32[27,3]{0,1:T(4,128)S(1)}, s32[27,3]{0,1:T(4,128)}, u32[]{:S(2)}) copy-start(s32[27,3]{0,1:T(4,128)} %param.5) | copy-start | bytes 976
  5.2 19.4 %collective-permute-start.5 = (bf16[12,32,1024]{2,1,0:T(8,128)(2,1)S(1)}, bf16[12,32,1024]{2,1,0:T(8,128)(2,1)}, u32[]{:S(2)}, u32[]{:S(2)}) collective-permute-start(bf16[12,32,1024]{2,1,0:T(8,128)(2,1)S(1)} %convert_element_type.30.rest_0_), channel_id=1, source_target_pairs={{0,2},{2,0},{1,3},{3,1},{4,6},{6,4},{5,7},{7,5},{8,10},{10,8},{9,1... | collective-permute-start | bytes 2359304 | tf_op jit(solution)/shard_map/ppermute | solution.py:21
  7.3 65.2 %collective-permute-start.4 = (bf16[12,32,1024]{2,1,0:T(8,128)(2,1)S(1)}, bf16[12,32,1024]{2,1,0:T(8,128)(2,1)}, u32[]{:S(2)}, u32[]{:S(2)}) collective-permute-start(bf16[12,32,1024]{2,1,0:T(8,128)(2,1)S(1)} %convert_element_type.30.rest_0_), channel_id=1, source_target_pairs={{0,1},{1,0},{2,3},{3,2},{4,5},{5,4},{6,7},{7,6},{8,9},{9,8},{10,11... | collective-permute-start | bytes 2359304 | tf_op jit(solution)/shard_map/ppermute | solution.py:21
  8.7 19.4 %copy-start.1 = (f32[54,4,512]{2,1,0:T(4,128)}, f32[54,4,512]{2,1,0:T(4,128)S(1)}, u32[]{:S(2)}) copy-start(f32[54,4,512]{2,1,0:T(4,128)S(1)} %reshape.166) | copy-start | bytes 1327108
  11.0 19.9 %collective-permute-start.3 = (bf16[1,54,512]{2,1,0:T(8,128)(2,1)}, bf16[1,54,512]{2,1,0:T(8,128)(2,1)S(1)}, u32[]{:S(2)}, u32[]{:S(2)}) collective-permute-start(bf16[1,54,512]{2,1,0:T(8,128)(2,1)} %slice.31), channel_id=1, source_target_pairs={{0,12},{4,0},{8,4},{12,8},{1,13},{5,1},{9,5},{13,9},{2,14},{6,2},{... | collective-permute-start | bytes 165896 | tf_op jit(solution)/shard_map/ppermute | solution.py:21
  15.3 22.9 %collective-permute-start.1 = (bf16[6,32,1024]{2,1,0:T(8,128)(2,1)}, bf16[6,32,1024]{2,1,0:T(8,128)(2,1)S(1)}, u32[]{:S(2)}, u32[]{:S(2)}) collective-permute-start(bf16[6,32,1024]{2,1,0:T(8,128)(2,1)} %get-tuple-element.13), channel_id=1, source_target_pairs={{0,12},{4,0},{8,4},{12,8},{1,13},{5,1},{9,5},{13,9},{2,14},{6,2},{... | collective-permute-start | bytes 1179656 | tf_op jit(solution)/shard_map/ppermute | solution.py:21
  15.5 22.7 %collective-permute-start = (bf16[6,32,1024]{2,1,0:T(8,128)(2,1)}, bf16[6,32,1024]{2,1,0:T(8,128)(2,1)}, u32[]{:S(2)}, u32[]{:S(2)}) collective-permute-start(bf16[6,32,1024]{2,1,0:T(8,128)(2,1)} %get-tuple-element.14), channel_id=1, source_target_pairs={{0,4},{4,8},{8,12},{12,0},{1,5},{5,9},{9,13},{13,1},{2,6},{6,10},{... | collective-permute-start | bytes 1179656 | tf_op jit(solution)/shard_map/ppermute | solution.py:21
  24.7 47.8 %collective-permute-start.6 = (bf16[12,32,1024]{2,1,0:T(8,128)(2,1)}, bf16[12,32,1024]{2,1,0:T(8,128)(2,1)}, u32[]{:S(2)}, u32[]{:S(2)}) collective-permute-start(bf16[12,32,1024]{2,1,0:T(8,128)(2,1)} %collective-permute-done.5.rest_2_), channel_id=1, source_target_pairs={{0,1},{1,0},{2,3},{3,2},{4,5},{5,4},{6,7},{7,6},{8,9},{9,8},{10,11... | collective-permute-start | bytes 2359304 | tf_op jit(solution)/shard_map/ppermute | solution.py:21
  30.9 7.3 %collective-permute-start.2 = (bf16[2,54,512]{2,1,0:T(8,128)(2,1)}, bf16[2,54,512]{2,1,0:T(8,128)(2,1)S(1)}, u32[]{:S(2)}, u32[]{:S(2)}) collective-permute-start(bf16[2,54,512]{2,1,0:T(8,128)(2,1)} %slice.30), channel_id=1, source_target_pairs={{0,4},{4,8},{8,12},{12,0},{1,5},{5,9},{9,13},{13,1},{2,6},{6,10},{... | collective-permute-start | bytes 331784 | tf_op jit(solution)/shard_map/ppermute | solution.py:21
  38.2 34.3 %copy-start = (f32[4,27,512]{2,1,0:T(8,128)S(1)}, f32[4,27,512]{2,1,0:T(8,128)}, u32[]{:S(2)}) copy-start(f32[4,27,512]{2,1,0:T(8,128)} %get-tuple-element.16.cos_ref) | copy-start | bytes 663556
  93.4 7.7 %collective-permute-start.7 = (bf16[64,864]{1,0:T(8,128)(2,1)S(1)}, bf16[64,864]{1,0:T(8,128)(2,1)S(1)}, u32[]{:S(2)}, u32[]{:S(2)}) collective-permute-start(bf16[64,864]{1,0:T(8,128)(2,1)S(1)} %get-tuple-element.9), channel_id=1, source_target_pairs={{0,0},{1,4},{2,8},{3,12},{4,1},{5,5},{6,9},{7,13},{8,2},{9,6},{10,... | collective-permute-start | bytes 331784 | tf_op jit(solution)/shard_map/ppermute | solution.py:391
  95.3 5.8 %collective-permute-start.8 = (bf16[64,864]{1,0:T(8,128)(2,1)S(1)}, bf16[64,864]{1,0:T(8,128)(2,1)S(1)}, u32[]{:S(2)}, u32[]{:S(2)}) collective-permute-start(bf16[64,864]{1,0:T(8,128)(2,1)S(1)} %get-tuple-element.10), channel_id=1, source_target_pairs={{0,1},{1,5},{2,9},{3,13},{4,2},{5,6},{6,10},{7,14},{8,3},{9,7},{10... | collective-permute-start | bytes 331784 | tf_op jit(solution)/shard_map/ppermute | solution.py:391
  95.4 12.1 %collective-permute-start.9 = (bf16[64,864]{1,0:T(8,128)(2,1)S(1)}, bf16[64,864]{1,0:T(8,128)(2,1)S(1)}, u32[]{:S(2)}, u32[]{:S(2)}) collective-permute-start(bf16[64,864]{1,0:T(8,128)(2,1)S(1)} %get-tuple-element.11), channel_id=1, source_target_pairs={{0,2},{1,6},{2,10},{3,14},{4,3},{5,7},{6,11},{7,15},{8,0},{9,4},{1... | collective-permute-start | bytes 331784 | tf_op jit(solution)/shard_map/ppermute | solution.py:391
  97.1 20.9 %collective-permute-start.10 = (bf16[64,864]{1,0:T(8,128)(2,1)S(1)}, bf16[64,864]{1,0:T(8,128)(2,1)S(1)}, u32[]{:S(2)}, u32[]{:S(2)}) collective-permute-start(bf16[64,864]{1,0:T(8,128)(2,1)S(1)} %get-tuple-element.12), channel_id=1, source_target_pairs={{0,3},{1,7},{2,11},{3,15},{4,0},{5,4},{6,8},{7,12},{8,1},{9,5},{10... | collective-permute-start | bytes 331784 | tf_op jit(solution)/shard_map/ppermute | solution.py:391

commit v2 on v1

--- a/solution.py
+++ b/solution.py
@@ -149,12 +149,12 @@
     return lax.psum_scatter(shares, "brick", scatter_dimension=3, tiled=True)
 
 
-def smear_kernel(planes, rows, x_ref, lo_ref, hi_ref, lk_ref, lb_ref, la_ref, out_ref, stage, table, f0, f1, moved):
+def smear_kernel(planes, rows, x_ref, lo_ref, hi_ref, lk_ref, out_ref, stage, table, f0, f1, moved):
     plane = LY * LZ
     f32 = jnp.float32
     blocks = rows // 8
-    depth = lax.broadcasted_iota(jnp.int32, (8, plane), 1) % LZ
-    link_depth = lax.broadcasted_iota(jnp.int32, (56, plane), 1) % LZ
+    depth = lax.broadcasted_iota(jnp.int32, (8, 128), 1) % LZ
+    link_depth = lax.broadcasted_iota(jnp.int32, (stage.shape[1], plane), 1) % LZ
 
     for k in range(6):
         f0[k] = lo_ref[k].astype(f32)
@@ -165,11 +165,13 @@
         return carry
 
     lax.fori_loop(0, 3 * planes, take, 0)
-    for k in range(2):
-        stage[k, 0:54] = lb_ref[k].astype(f32)
+    for j in range(stage.shape[1] // rows):
+        at = slice(j * rows, (j + 1) * rows)
+        stage[0, at] = lo_ref[6 + j, :, 0:plane].astype(f32)
+        stage[1, at] = lo_ref[6 + j, :, plane:].astype(f32)
+        stage[2 + planes, at] = hi_ref[6 + j, :, 0:plane].astype(f32)
     for k in range(planes):
-        stage[2 + k, 0:54] = lk_ref[k]
-    stage[2 + planes, 0:54] = la_ref[0].astype(f32)
+        stage[2 + k, 0:54] = lk_ref[:, k * plane : (k + 1) * plane]
 
     def spread(t, carry):
         here = stage[t + 1]
@@ -188,60 +190,66 @@
 
     def one_plane(source, at, links, target, to):
         def shift(k, carry):
-            c, b = k // blocks, k % blocks
-            rows_at = pl.ds(pl.multiple_of(b * 8, 8), 8)
-            for half in range(2):
-                lanes = slice(half * plane, (half + 1) * plane)
+            c, half = k // 2, k % 2
+            for b in range(blocks):
+                rows_at = slice(b * 8, b * 8 + 8)
+                lanes = pl.ds(pl.multiple_of(half * plane, plane), plane)
                 v = source[at * 3 + c, rows_at, lanes]
                 moved[0, c, rows_at, lanes] = pltpu.roll(v, plane - LZ, 1)
                 moved[1, c, rows_at, lanes] = pltpu.roll(v, LZ, 1)
-                moved[2, c, rows_at, lanes] = jnp.where(
-                    depth == LZ - 1, pltpu.roll(v, LZ - 1, 1), pltpu.roll(v, plane - 1, 1)
-                )
-                moved[3, c, rows_at, lanes] = jnp.where(
-                    depth == 0, pltpu.roll(v, plane - (LZ - 1), 1), pltpu.roll(v, 1, 1)
-                )
+                for part in range(plane // 128):
+                    w = v[:, part * 128 : part * 128 + 128]
+                    here = pl.ds(pl.multiple_of(half * plane + part * 128, 128), 128)
+                    moved[2, c, rows_at, here] = jnp.where(
+                        depth == LZ - 1, pltpu.roll(w, LZ - 1, 1), pltpu.roll(w, 127, 1)
+                    )
+                    moved[3, c, rows_at, here] = jnp.where(
+                        depth == 0, pltpu.roll(w, 128 - (LZ - 1), 1), pltpu.roll(w, 1, 1)
+                    )
             return carry
 
-        lax.fori_loop(0, 3 * blocks, shift, 0)
-
-        def block(k, carry):
-            b, lane = k % blocks, k // blocks
-            rows_at = pl.ds(pl.multiple_of(b * 8, 8), 8)
-            real_at = pl.ds(pl.multiple_of(lane * 128, 128), 128)
-            imag_at = pl.ds(pl.multiple_of(plane + lane * 128, 128), 128)
-            acc = [[None, None] for _ in range(3)]
-
-            def add(r, part, value):
-                acc[r][part] = value if acc[r][part] is None else acc[r][part] + value
+        lax.fori_loop(0, 6, shift, 0)
+
+        def block(lane, carry):
+            lanes = (
+                pl.ds(pl.multiple_of(lane * 128, 128), 128),
+                pl.ds(pl.multiple_of(plane + lane * 128, 128), 128),
+            )
+            acc = {}
+
+            def add(b, r, part, value):
+                acc[b, r, part] = value + acc[b, r, part] if (b, r, part) in acc else value
 
             for way in range(6):
                 direction, back = way // 2, way % 2
                 for c in range(3):
-                    if direction == 0:
-                        index = (at + 1 - 2 * back) * 3 + c
-                        sr = source[index, rows_at, real_at]
-                        si = source[index, rows_at, imag_at]
-                    else:
-                        sr = moved[way - 2, c, rows_at, real_at]
-                        si = moved[way - 2, c, rows_at, imag_at]
+                    pair = []
                     for r in range(3):
                         row = direction * 18 + (54 + c * 6 + r * 2 if back else r * 6 + c * 2)
-                        ur = table[links, row, :, real_at]
-                        ui = table[links, row + 1, :, real_at]
-                        if back:
-                            add(r, 0, ur * sr + ui * si)
-                            add(r, 1, ur * si - ui * sr)
+                        pair.append((table[links, row, :, lanes[0]], table[links, row + 1, :, lanes[0]]))
+                    for b in range(blocks):
+                        at_rows = slice(b * 8, b * 8 + 8)
+                        if direction == 0:
+                            index = (at + 1 - 2 * back) * 3 + c
+                            sr = source[index, at_rows, lanes[0]]
+                            si = source[index, at_rows, lanes[1]]
                         else:
-                            add(r, 0, ur * sr - ui * si)
-                            add(r, 1, ur * si + ui * sr)
-            for r in range(3):
-                for part, lanes in ((0, real_at), (1, imag_at)):
-                    mid = source[at * 3 + r, rows_at, lanes]
-                    target[to * 3 + r, rows_at, lanes] = mid + KAPPA * (acc[r][part] - 6.0 * mid)
+                            sr = moved[way - 2, c, at_rows, lanes[0]]
+                            si = moved[way - 2, c, at_rows, lanes[1]]
+                        for r, (ur, ui) in enumerate(pair):
+                            if back:
+                                add(b, r, 0, ur * sr + ui * si)
+                                add(b, r, 1, ur * si - ui * sr)
+                            else:
+                                add(b, r, 0, ur * sr - ui * si)
+                                add(b, r, 1, ur * si + ui * sr)
+            for (b, r, part), value in acc.items():
+                at_rows = slice(b * 8, b * 8 + 8)
+                mid = source[at * 3 + r, at_rows, lanes[part]]
+                target[to * 3 + r, at_rows, lanes[part]] = mid + KAPPA * (value - 6.0 * mid)
             return carry
 
-        lax.fori_loop(0, blocks * (plane // 128), block, 0)
+        lax.fori_loop(0, plane // 128, block, 0)
 
     def first(t, carry):
         one_plane(f0, t + 1, t, f1, t)
@@ -266,35 +274,57 @@
     plane = LY * LZ
     raw_refs = rest[:groups]
     out_refs = rest[groups : 2 * groups]
-    right, left, wide, total = rest[2 * groups :]
+    sides = (rest[2 * groups : 2 * groups + 2], rest[2 * groups + 2 : 2 * groups + 4])
+    total = rest[2 * groups + 4]
+    chunks = smeared_ref.shape[0]
     total[...] = jnp.zeros_like(total)
-
-    def chunk(k, carry):
+    per = max(1, 256 // rows)
+
+    def fill(k, right):
         for u in range(groups):
             raw = raw_refs[u][k]
             first = 2 * rows * u
             right[first : first + rows, :] = raw
             right[first + rows : first + 2 * rows, 0:plane] = -raw[:, plane:]
             right[first + rows : first + 2 * rows, plane:] = raw[:, :plane]
-        wide[...] = smeared_ref[k].astype(jnp.float32)
-
-        def turn(q, carry):
-            cosine = cos_ref[k // 3, pl.ds(q, 1), :]
-            sine = sin_ref[k // 3, pl.ds(q, 1), :]
-            sr = wide[:, 0:plane]
-            si = wide[:, plane:]
-            at = pl.ds(pl.multiple_of(q * rows, rows), rows)
-            left[at, 0:plane] = (cosine * sr + sine * si).astype(left.dtype)
-            left[at, plane:] = (cosine * si - sine * sr).astype(left.dtype)
-            return carry
-
-        lax.fori_loop(0, count, turn, 0)
-        total[...] += lax.dot_general(
-            right[...], left[...], (((1,), (1,)), ((), ())), preferred_element_type=jnp.float32
-        )
-        return carry
-
-    lax.fori_loop(0, smeared_ref.shape[0], chunk, 0)
+
+    def turn(k, left, q):
+        for lane in range(0, plane, 128):
+            cosine = cos_ref[k // 3, q : q + 1, lane : lane + 128]
+            sine = sin_ref[k // 3, q : q + 1, lane : lane + 128]
+            for row in range(0, rows, 16):
+                sr = smeared_ref[k, row : row + 16, lane : lane + 128].astype(jnp.float32)
+                si = smeared_ref[k, row : row + 16, plane + lane : plane + lane + 128].astype(jnp.float32)
+                at = slice(q * rows + row, q * rows + row + 16)
+                left[at, lane : lane + 128] = (cosine * sr + sine * si).astype(left.dtype)
+                left[at, plane + lane : plane + lane + 128] = (cosine * si - sine * sr).astype(left.dtype)
+
+    def stage(k, side, later, other):
+        right, left = side
+        for q0 in range(0, count, per):
+            q1 = min(q0 + per, count)
+            at = slice(q0 * rows, q1 * rows)
+            part = lax.dot_general(
+                right[...], left[at, :], (((1,), (1,)), ((), ())), preferred_element_type=jnp.float32
+            )
+            for q in range(q0, q1):
+                turn(later, other[1], q)
+            total[:, at] += part
+        fill(later, other[0])
+
+    fill(0, sides[0][0])
+    for q in range(count):
+        turn(0, sides[0][1], q)
+
+    def two(h, carry):
+        k = 2 * h
+        stage(k, sides[0], jnp.minimum(k + 1, chunks - 1), sides[1])
+        stage(k + 1, sides[1], jnp.minimum(k + 2, chunks - 1), sides[0])
+        return carry
+
+    lax.fori_loop(0, chunks // 2, two, 0)
+    if chunks % 2:
+        stage(chunks - 1, sides[0], chunks - 1, sides[1])
     for k in range(groups):
         first = pl.multiple_of(order_ref[k] * (2 * rows), 2 * rows)
         out_refs[k][...] = (total[pl.ds(first, 2 * rows), :] * scale).astype(out_refs[k].dtype)
@@ -324,27 +354,26 @@
     wide = jnp.transpose(vectors.reshape((rows, 3, 2, planes, plane)), (3, 1, 0, 2, 4))
     wide = wide.reshape((planes * 3, rows, 2 * plane))
     raw = wide.astype(low)
-    below = from_behind(raw[-6:], "brick", 1)
-    above = from_behind(raw[:6], "brick", -1)
-    links = jnp.transpose(gauge_links.reshape((54, planes, plane)), (1, 0, 2))
-    links_low = links.astype(low)
-    links_below = from_behind(links_low[-2:], "brick", 1)
-    links_above = from_behind(links_low[:1], "brick", -1)
-    gathered = []
-    for kv in range(vecs):
-        one = raw if kv == 0 else from_behind(raw, "vec", -kv)
-        for ks in range(subs):
-            gathered.append(one if ks == 0 else from_behind(one, "sub", -ks))
+    links = gauge_links.reshape((54, local_sites))
+    fold = -(-54 // rows)
+
+    def with_links(part, piece):
+        piece = jnp.pad(piece.astype(low), ((0, fold * rows - 54), (0, 0)))
+        return jnp.concatenate([part, piece.reshape((fold, rows, 2 * plane))], axis=0)
+
+    below = from_behind(with_links(raw[-6:], links[:, -2 * plane :]), "brick", 1)
+    above = from_behind(with_links(raw[:6], links[:, : 2 * plane]), "brick", -1)
+    across = [raw] + [from_behind(raw, "vec", -kv) for kv in range(1, vecs)]
     cosines, sines = phase_tables(momenta, local_sites, bricks * planes)
 
     vmem = pl.BlockSpec(memory_space=pltpu.VMEM)
     smeared = pl.pallas_call(
         functools.partial(smear_kernel, planes, rows),
         out_shape=jax.ShapeDtypeStruct((planes * 3, rows, 2 * plane), low),
-        in_specs=[vmem] * 6,
+        in_specs=[vmem] * 4,
         out_specs=vmem,
         scratch_shapes=[
-            pltpu.VMEM((planes + 3, 56, plane), jnp.float32),
+            pltpu.VMEM((planes + 3, fold * rows, plane), jnp.float32),
             pltpu.VMEM((planes + 2, 108, 8, plane), jnp.float32),
             pltpu.VMEM(((planes + 4) * 3, rows, 2 * plane), jnp.float32),
             pltpu.VMEM(((planes + 2) * 3, rows, 2 * plane), jnp.float32),
@@ -355,7 +384,12 @@
             flops=432 * 2 * (planes + 1) * plane * rows * 4, bytes_accessed=4 * 2**20, transcendentals=0
         ),
         name="smear",
-    )(wide, below, above, links, links_below, links_above)
+    )(wide, below, above, links)
+    *across, smeared = lax.optimization_barrier((*across, smeared))
+    gathered = []
+    for one in across:
+        for ks in range(subs):
+            gathered.append(one if ks == 0 else from_behind(one, "sub", -ks))
 
     me_vec, me_sub, me_brick = (lax.axis_index(a) for a in ("vec", "sub", "brick"))
     owner = (me_brick + lax.iota(jnp.int32, groups)) % groups
@@ -369,7 +403,8 @@
         scratch_shapes=[
             pltpu.VMEM((2 * rows * groups, 2 * plane), low),
             pltpu.VMEM((count * rows, 2 * plane), low),
-            pltpu.VMEM((rows, 2 * plane), jnp.float32),
+            pltpu.VMEM((2 * rows * groups, 2 * plane), low),
+            pltpu.VMEM((count * rows, 2 * plane), low),
             pltpu.VMEM((2 * rows * groups, count * rows), jnp.float32),
         ],
         compiler_params=pltpu.CompilerParams(vmem_limit_bytes=40 * 2**20),

time: 120 us -> 110 us (0.917)
  Pallas kernels: 55.2 us -> 42.3 us
  waiting for transfers between devices: 30.5 us -> 41.7 us
  starting transfers between devices: 18.3 us -> 13 us
  local copies, waits for them, and re-layouts: 13.5 us -> 9.26 us
    ppermute x7 -> x5, waiting for transfers between devices: 13.7 us -> 24.5 us  [from_behind(): lax.ppermute(array, axis, [(i, (i + by) % peers) for i in range(peers)])]
    pallas_call x1, Pallas kernels: 20.9 us -> 13.1 us  [shards_kernels(): pl.pallas_call(functools.partial(product_kernel, groups, rows, count, sca...]
    pallas_call x1, Pallas kernels: 34.3 us -> 29.2 us  [shards_kernels(): pl.pallas_call(functools.partial(smear_kernel, planes, rows), out_shape=j...]
    ppermute x7 -> x5, starting transfers between devices: 10.6 us -> 6.09 us  [from_behind(): lax.ppermute(array, axis, [(i, (i + by) % peers) for i in range(peers)])]
    slice x3 -> x2, local copies, waits for them, and re-layouts: 3.95 us -> 0.85 us  [shards_kernels(): above = from_behind(with_links(raw[:6], links[:, :2 * plane]), 'brick', -1)]
    concatenate x0 -> x2, other arithmetic: none -> 1.7 us  [with_links(): jnp.concatenate([part, piece.reshape((fold, rows, 2 * plane))], axis=0)]
    reshape x3 -> x1, local copies, waits for them, and re-layouts: 2.42 us -> 1.32 us  [shards_kernels(): links = gauge_links.reshape((54, local_sites))]
  transfers between devices with their start and end apart: 11 -> 9, of which waited for: 4 -> 6; matrix products, arithmetic and copies ran while one was open for 7% -> 5% of each run, Pallas kernels for 29% -> 27%
where the time goes in v2:
time: 110 us
  Pallas kernels  42.3 us (38%)
  waiting for transfers between devices  41.7 us (38%)
  starting transfers between devices  13 us (12%)
  local copies, waits for them, and re-layouts  9.26 us (8%)
  other arithmetic  3.34 us (3%)
    pallas_call x1, Pallas kernels, shards_kernels(): pl.pallas_call(functools.partial(smear_kernel, planes, rows), out_shape=j...  29.2 us
    ppermute x5, waiting for transfers between devices, from_behind(): lax.ppermute(array, axis, [(i, (i + by) % peers) for i in range(peers)])  24.5 us
    ppermute x4, waiting for transfers between devices, shards_kernels(): lax.ppermute(blocks[k], ('brick', 'vec', 'sub'), pairs).astype(jnp.float32)  17.2 us
    pallas_call x1, Pallas kernels, shards_kernels(): pl.pallas_call(functools.partial(product_kernel, groups, rows, count, sca...  13.1 us
    ppermute x4, starting transfers between devices, shards_kernels(): lax.ppermute(blocks[k], ('brick', 'vec', 'sub'), pairs).astype(jnp.float32)  6.95 us
    ppermute x5, starting transfers between devices, from_behind(): lax.ppermute(array, axis, [(i, (i + by) % peers) for i in range(peers)])  6.09 us
    reshape x2, local copies, waits for them, and re-layouts, shards_kernels(): vectors.reshape((rows, 3, 2, planes, plane))  3.71 us
  transfers between devices with their start and end apart: 9, of which 6 were waited for; matrix products, arithmetic and copies ran while one was open for 5% of the time, Pallas kernels for 27%

profile of v2, /device:TPU:1, one launch (start us, length us, event | category | flops | bytes accessed | tf_op | source)
XLA Modules:
  0.0 109.8 jit_solution(9035762758215184147)
XLA Ops:
  0.0 2.9 %reshape.170 = f32[32,3,2,4,512]{4,3,2,1,0:T(4,128)S(1)} reshape(f32[32,3,2,2048]{3,2,1,0:T(2,128)} %param.3) | data formatting | bytes 3145728 | tf_op jit(solution)/shard_map/reshape | solution.py:354
  2.9 0.8 copy.9
  3.7 1.4 %reshape.171.x_ref = f32[12,32,1024]{2,1,0:T(8,128)S(1)} reshape(f32[4,3,32,2,512]{4,3,2,1,0:T(2,128)S(1)} %bitcast.12) | data formatting | bytes 3145728 | tf_op jit(solution)/shard_map/reshape | solution.py:355
  5.1 0.1 convert_element_type.32.rest_0_
  5.2 2.1 %collective-permute-start = (bf16[12,32,1024]{2,1,0:T(8,128)(2,1)S(1)}, bf16[12,32,1024]{2,1,0:T(8,128)(2,1)}, u32[]{:S(2)}, u32[]{:S(2)}) collective-permute-start(bf16[12,32,1024]{2,1,0:T(8,128)(2,1)S(1)} %convert_element_type.32.rest_0_), channel_id=1, source_target_pairs={{0,2},{2,0},{1,3},{3,1},{4,6},{6,4},{5,7},{7,5},{8,10},{10,8},{9,1... | collective-permute-start | bytes 2359304 | tf_op jit(solution)/shard_map/ppermute | solution.py:21
  7.3 0.8 fusion.23
  8.1 1.3 %reshape.172.lk_ref = f32[54,2048]{1,0:T(8,128)S(1)} reshape(f32[3,3,3,2,2048]{4,3,2,1,0:T(2,128)} %param.4) | data formatting | bytes 884736 | tf_op jit(solution)/shard_map/reshape | solution.py:357
  9.5 0.8 pad_maximum_fusion
  10.4 1.3 %collective-permute-start.1 = (bf16[8,32,1024]{2,1,0:T(8,128)(2,1)}, bf16[8,32,1024]{2,1,0:T(8,128)(2,1)S(1)}, u32[]{:S(2)}, u32[]{:S(2)}) collective-permute-start(bf16[8,32,1024]{2,1,0:T(8,128)(2,1)} %pad_maximum_fusion), channel_id=1, source_target_pairs={{0,4},{4,8},{8,12},{12,0},{1,5},{5,9},{9,13},{13,1},{2,6},{6,10},{... | collective-permute-start | bytes 1572872 | tf_op jit(solution)/shard_map/ppermute | solution.py:21
  11.7 0.9 pad_maximum_fusion.1
  12.6 2.1 %collective-permute-start.2 = (bf16[8,32,1024]{2,1,0:T(8,128)(2,1)}, bf16[8,32,1024]{2,1,0:T(8,128)(2,1)}, u32[]{:S(2)}, u32[]{:S(2)}) collective-permute-start(bf16[8,32,1024]{2,1,0:T(8,128)(2,1)} %pad_maximum_fusion.1), channel_id=1, source_target_pairs={{0,12},{4,0},{8,4},{12,8},{1,13},{5,1},{9,5},{13,9},{2,14},{6,2},{... | collective-permute-start | bytes 1572872 | tf_op jit(solution)/shard_map/ppermute | solution.py:21
  14.6 10.4 %collective-permute-done.1.lo_ref = bf16[8,32,1024]{2,1,0:T(8,128)(2,1)S(1)} collective-permute-done((bf16[8,32,1024]{2,1,0:T(8,128)(2,1)}, bf16[8,32,1024]{2,1,0:T(8,128)(2,1)S(1)}, u32[]{:S(2)}, u32[]{:S(2)}) %collective-permute-start.1) | collective-permute-done | bytes 524320 | tf_op jit(solution)/shard_map/ppermute | solution.py:21
  25.1 12.6 %collective-permute-done.2.hi_ref = bf16[8,32,1024]{2,1,0:T(8,128)(2,1)} collective-permute-done((bf16[8,32,1024]{2,1,0:T(8,128)(2,1)}, bf16[8,32,1024]{2,1,0:T(8,128)(2,1)}, u32[]{:S(2)}, u32[]{:S(2)}) %collective-permute-start.2) | collective-permute-done | bytes 524320 | tf_op jit(solution)/shard_map/ppermute | solution.py:21
  37.6 29.2 %smear.1.smeared_ref = bf16[12,32,1024]{2,1,0:T(8,128)(2,1)S(1)} custom-call(f32[12,32,1024]{2,1,0:T(8,128)S(1)} %reshape.171.x_ref, bf16[8,32,1024]{2,1,0:T(8,128)(2,1)S(1)} %collective-permute-done.1.lo_ref, bf16[8,32,1024]{2,1,0:T(8,128)(2,1)} %collective-permute-done.2.hi_ref, f32[54,2048]{1,0:T(8,128)S(1)} %reshape.172.lk_ref), custom_call_target="tpu_custom_call" | custom-call | flops 283115520 | bytes 4194304 | tf_op jit(solution)/shard_map/smear/pallas_call | solution.py:370
  66.8 0.0 collective-permute-done.rest_2_
  66.8 0.6 collective-permute-start.3
  67.4 0.1 collective-permute-start.4
  67.6 1.4 %fusion.12 = (f32[4,27,512]{2,1,0:T(8,128)S(1)}, f32[4,27,512]{2,1,0:T(8,128)S(1)}) fusion(s32[4,512]{1,0:T(4,128)S(1)} %get-tuple-element.28, s32[27]{0:T(128)S(1)} %get-tuple-element.26, s32[4,512]{1,0:T(4,128)S(1)} %get-tuple-element.29, s32[27]{0:T(128)S(1)} %get-tuple-element.27, s32[4,512]{1,0:T(4,128)S(1)} %add_select_fusion.6, ...), kind=kLoop, calls=%fused_computation.31 | loop fusion | flops 2488320 | bytes 467268 | tf_op jit(solution)/shard_map/sin | solution.py:343
  68.9 0.4 collective-permute-done.3.rest_1_
  69.3 1.1 %collective-permute-done.4.rest_3_ = bf16[12,32,1024]{2,1,0:T(8,128)(2,1)S(1)} collective-permute-done((bf16[12,32,1024]{2,1,0:T(8,128)(2,1)}, bf16[12,32,1024]{2,1,0:T(8,128)(2,1)S(1)}, u32[]{:S(2)}, u32[]{:S(2)}) %collective-permute-start.4) | collective-permute-done | bytes 786464 | tf_op jit(solution)/shard_map/ppermute | solution.py:21
  70.4 13.1 %product.1 = (bf16[64,864]{1,0:T(8,128)(2,1)S(1)}, bf16[64,864]{1,0:T(8,128)(2,1)S(1)}, bf16[64,864]{1,0:T(8,128)(2,1)S(1)}, bf16[64,864]{1,0:T(8,128)(2,1)S(1)}) custom-call(s32[4]{0:T(128)S(1)} %fusion.17.order_ref, f32[4,27,512]{2,1,0:T(8,128)S(1)} %get-tuple-element.24.cos_ref, f32[4,27,512]{2,1,0:T(8,128)S(1)} %get-tuple-element.23.sin_ref, ...), custom_call_target="tpu_custom_call" | custom-call | flops 5435817984 | bytes 8388608 | tf_op jit(solution)/shard_map/product/pallas_call | solution.py:398
  83.5 2.5 %collective-permute-start.5 = (bf16[64,864]{1,0:T(8,128)(2,1)S(1)}, bf16[64,864]{1,0:T(8,128)(2,1)S(1)}, u32[]{:S(2)}, u32[]{:S(2)}) collective-permute-start(bf16[64,864]{1,0:T(8,128)(2,1)S(1)} %get-tuple-element.15), channel_id=1, source_target_pairs={{0,0},{1,4},{2,8},{3,12},{4,1},{5,5},{6,9},{7,13},{8,2},{9,6},{10,... | collective-permute-start | bytes 331784 | tf_op jit(solution)/shard_map/ppermute | solution.py:426
  86.0 0.1 collective-permute-start.6
  86.1 1.3 %collective-permute-start.7 = (bf16[64,864]{1,0:T(8,128)(2,1)S(1)}, bf16[64,864]{1,0:T(8,128)(2,1)S(1)}, u32[]{:S(2)}, u32[]{:S(2)}) collective-permute-start(bf16[64,864]{1,0:T(8,128)(2,1)S(1)} %get-tuple-element.17), channel_id=1, source_target_pairs={{0,2},{1,6},{2,10},{3,14},{4,3},{5,7},{6,11},{7,15},{8,0},{9,4},{1... | collective-permute-start | bytes 331784 | tf_op jit(solution)/shard_map/ppermute | solution.py:426
  87.4 3.1 %collective-permute-start.8 = (bf16[64,864]{1,0:T(8,128)(2,1)S(1)}, bf16[64,864]{1,0:T(8,128)(2,1)S(1)}, u32[]{:S(2)}, u32[]{:S(2)}) collective-permute-start(bf16[64,864]{1,0:T(8,128)(2,1)S(1)} %get-tuple-element.18), channel_id=1, source_target_pairs={{0,3},{1,7},{2,11},{3,15},{4,0},{5,4},{6,8},{7,12},{8,1},{9,5},{10... | collective-permute-start | bytes 331784 | tf_op jit(solution)/shard_map/ppermute | solution.py:426
  90.5 0.0 collective-permute-done.5
  90.5 0.0 collective-permute-done.6
  90.5 7.0 %collective-permute-done.7 = bf16[64,864]{1,0:T(8,128)(2,1)S(1)} collective-permute-done((bf16[64,864]{1,0:T(8,128)(2,1)S(1)}, bf16[64,864]{1,0:T(8,128)(2,1)S(1)}, u32[]{:S(2)}, u32[]{:S(2)}) %collective-permute-start.7) | collective-permute-done | bytes 110624 | tf_op jit(solution)/shard_map/ppermute | solution.py:426
  97.5 10.3 %collective-permute-done.8 = bf16[64,864]{1,0:T(8,128)(2,1)S(1)} collective-permute-done((bf16[64,864]{1,0:T(8,128)(2,1)S(1)}, bf16[64,864]{1,0:T(8,128)(2,1)S(1)}, u32[]{:S(2)}, u32[]{:S(2)}) %collective-permute-start.8) | collective-permute-done | bytes 110624 | tf_op jit(solution)/shard_map/ppermute | solution.py:426
  107.7 0.1 convert_add_fusion
  107.8 0.4 reshape.175
  108.2 1.6 %copy.7 = f32[32,27,2,32]{3,2,1,0:T(2,128)} copy(f32[32,27,2,32]{3,1,0,2:T(8,128)S(1)} %bitcast.13) | data formatting | bytes 442368 | tf_op jit(solution)/shard_map/transpose | solution.py:428
  (12 shorter events, 0.2 us)
Async XLA Ops:
  5.2 61.6 %collective-permute-start = (bf16[12,32,1024]{2,1,0:T(8,128)(2,1)S(1)}, bf16[12,32,1024]{2,1,0:T(8,128)(2,1)}, u32[]{:S(2)}, u32[]{:S(2)}) collective-permute-start(bf16[12,32,1024]{2,1,0:T(8,128)(2,1)S(1)} %convert_element_type.32.rest_0_), channel_id=1, source_target_pairs={{0,2},{2,0},{1,3},{3,1},{4,6},{6,4},{5,7},{7,5},{8,10},{10,8},{9,1... | collective-permute-start | bytes 2359304 | tf_op jit(solution)/shard_map/ppermute | solution.py:21
  9.5 2.2 %copy-start = (bf16[6,32,1024]{2,1,0:T(8,128)(2,1)S(1)}, bf16[6,32,1024]{2,1,0:T(8,128)(2,1)}, u32[]{:S(2)}) copy-start(bf16[6,32,1024]{2,1,0:T(8,128)(2,1)} %get-tuple-element.19) | copy-start | bytes 1179652
  10.4 14.7 %collective-permute-start.1 = (bf16[8,32,1024]{2,1,0:T(8,128)(2,1)}, bf16[8,32,1024]{2,1,0:T(8,128)(2,1)S(1)}, u32[]{:S(2)}, u32[]{:S(2)}) collective-permute-start(bf16[8,32,1024]{2,1,0:T(8,128)(2,1)} %pad_maximum_fusion), channel_id=1, source_target_pairs={{0,4},{4,8},{8,12},{12,0},{1,5},{5,9},{9,13},{13,1},{2,6},{6,10},{... | collective-permute-start | bytes 1572872 | tf_op jit(solution)/shard_map/ppermute | solution.py:21
  12.6 25.1 %collective-permute-start.2 = (bf16[8,32,1024]{2,1,0:T(8,128)(2,1)}, bf16[8,32,1024]{2,1,0:T(8,128)(2,1)}, u32[]{:S(2)}, u32[]{:S(2)}) collective-permute-start(bf16[8,32,1024]{2,1,0:T(8,128)(2,1)} %pad_maximum_fusion.1), channel_id=1, source_target_pairs={{0,12},{4,0},{8,4},{12,8},{1,13},{5,1},{9,5},{13,9},{2,14},{6,2},{... | collective-permute-start | bytes 1572872 | tf_op jit(solution)/shard_map/ppermute | solution.py:21
  14.6 52.9 %copy-start.1 = (s32[27,3]{0,1:T(4,128)S(1)}, s32[27,3]{0,1:T(4,128)}, u32[]{:S(2)}) copy-start(s32[27,3]{0,1:T(4,128)} %param.5) | copy-start | bytes 976
  66.8 2.5 %collective-permute-start.3 = (bf16[12,32,1024]{2,1,0:T(8,128)(2,1)S(1)}, bf16[12,32,1024]{2,1,0:T(8,128)(2,1)S(1)}, u32[]{:S(2)}, u32[]{:S(2)}) collective-permute-start(bf16[12,32,1024]{2,1,0:T(8,128)(2,1)S(1)} %convert_element_type.32.rest_0_), channel_id=1, source_target_pairs={{0,1},{1,0},{2,3},{3,2},{4,5},{5,4},{6,7},{7,6},{8,9},{9,8},{10,11... | collective-permute-start | bytes 2359304 | tf_op jit(solution)/shard_map/ppermute | solution.py:21
  67.4 3.0 %collective-permute-start.4 = (bf16[12,32,1024]{2,1,0:T(8,128)(2,1)}, bf16[12,32,1024]{2,1,0:T(8,128)(2,1)S(1)}, u32[]{:S(2)}, u32[]{:S(2)}) collective-permute-start(bf16[12,32,1024]{2,1,0:T(8,128)(2,1)} %collective-permute-done.rest_2_), channel_id=1, source_target_pairs={{0,1},{1,0},{2,3},{3,2},{4,5},{5,4},{6,7},{7,6},{8,9},{9,8},{10,11... | collective-permute-start | bytes 2359304 | tf_op jit(solution)/shard_map/ppermute | solution.py:21
  83.5 7.0 %collective-permute-start.5 = (bf16[64,864]{1,0:T(8,128)(2,1)S(1)}, bf16[64,864]{1,0:T(8,128)(2,1)S(1)}, u32[]{:S(2)}, u32[]{:S(2)}) collective-permute-start(bf16[64,864]{1,0:T(8,128)(2,1)S(1)} %get-tuple-element.15), channel_id=1, source_target_pairs={{0,0},{1,4},{2,8},{3,12},{4,1},{5,5},{6,9},{7,13},{8,2},{9,6},{10,... | collective-permute-start | bytes 331784 | tf_op jit(solution)/shard_map/ppermute | solution.py:426
  86.0 4.5 %collective-permute-start.6 = (bf16[64,864]{1,0:T(8,128)(2,1)S(1)}, bf16[64,864]{1,0:T(8,128)(2,1)S(1)}, u32[]{:S(2)}, u32[]{:S(2)}) collective-permute-start(bf16[64,864]{1,0:T(8,128)(2,1)S(1)} %get-tuple-element.16), channel_id=1, source_target_pairs={{0,1},{1,5},{2,9},{3,13},{4,2},{5,6},{6,10},{7,14},{8,3},{9,7},{10... | collective-permute-start | bytes 331784 | tf_op jit(solution)/shard_map/ppermute | solution.py:426
  86.1 11.4 %collective-permute-start.7 = (bf16[64,864]{1,0:T(8,128)(2,1)S(1)}, bf16[64,864]{1,0:T(8,128)(2,1)S(1)}, u32[]{:S(2)}, u32[]{:S(2)}) collective-permute-start(bf16[64,864]{1,0:T(8,128)(2,1)S(1)} %get-tuple-element.17), channel_id=1, source_target_pairs={{0,2},{1,6},{2,10},{3,14},{4,3},{5,7},{6,11},{7,15},{8,0},{9,4},{1... | collective-permute-start | bytes 331784 | tf_op jit(solution)/shard_map/ppermute | solution.py:426
  87.4 20.3 %collective-permute-start.8 = (bf16[64,864]{1,0:T(8,128)(2,1)S(1)}, bf16[64,864]{1,0:T(8,128)(2,1)S(1)}, u32[]{:S(2)}, u32[]{:S(2)}) collective-permute-start(bf16[64,864]{1,0:T(8,128)(2,1)S(1)} %get-tuple-element.18), channel_id=1, source_target_pairs={{0,3},{1,7},{2,11},{3,15},{4,0},{5,4},{6,8},{7,12},{8,1},{9,5},{10... | collective-permute-start | bytes 331784 | tf_op jit(solution)/shard_map/ppermute | solution.py:426

commit v3 on v2

--- a/solution.py
+++ b/solution.py
@@ -149,7 +149,7 @@
     return lax.psum_scatter(shares, "brick", scatter_dimension=3, tiled=True)
 
 
-def smear_kernel(planes, rows, x_ref, lo_ref, hi_ref, lk_ref, out_ref, stage, table, f0, f1, moved):
+def smear_kernel(planes, rows, x_ref, lo_ref, hi_ref, lk_ref, out_ref, stage, table, f0, f1, moved_even, moved_odd):
     plane = LY * LZ
     f32 = jnp.float32
     blocks = rows // 8
@@ -188,80 +188,93 @@
 
     lax.fori_loop(0, planes + 2, spread, 0)
 
-    def one_plane(source, at, links, target, to):
-        def shift(k, carry):
-            c, half = k // 2, k % 2
-            for b in range(blocks):
-                rows_at = slice(b * 8, b * 8 + 8)
-                lanes = pl.ds(pl.multiple_of(half * plane, plane), plane)
-                v = source[at * 3 + c, rows_at, lanes]
-                moved[0, c, rows_at, lanes] = pltpu.roll(v, plane - LZ, 1)
-                moved[1, c, rows_at, lanes] = pltpu.roll(v, LZ, 1)
-                for part in range(plane // 128):
-                    w = v[:, part * 128 : part * 128 + 128]
-                    here = pl.ds(pl.multiple_of(half * plane + part * 128, 128), 128)
-                    moved[2, c, rows_at, here] = jnp.where(
-                        depth == LZ - 1, pltpu.roll(w, LZ - 1, 1), pltpu.roll(w, 127, 1)
-                    )
-                    moved[3, c, rows_at, here] = jnp.where(
-                        depth == 0, pltpu.roll(w, 128 - (LZ - 1), 1), pltpu.roll(w, 1, 1)
-                    )
+    half_blocks = blocks // 2
+
+    def shift(source, at, k, moved):
+        rows_at = pl.ds(pl.multiple_of(k % blocks * 8, 8), 8)
+        first_lane = k // blocks * plane
+        lanes = pl.ds(pl.multiple_of(first_lane, plane), plane)
+        for c in range(3):
+            v = source[at * 3 + c, rows_at, lanes]
+            moved[0, c, rows_at, lanes] = pltpu.roll(v, plane - LZ, 1)
+            moved[1, c, rows_at, lanes] = pltpu.roll(v, LZ, 1)
+            for part in range(plane // 128):
+                w = v[:, part * 128 : part * 128 + 128]
+                here = pl.ds(pl.multiple_of(first_lane + part * 128, 128), 128)
+                moved[2, c, rows_at, here] = jnp.where(
+                    depth == LZ - 1, pltpu.roll(w, LZ - 1, 1), pltpu.roll(w, 127, 1)
+                )
+                moved[3, c, rows_at, here] = jnp.where(
+                    depth == 0, pltpu.roll(w, 128 - (LZ - 1), 1), pltpu.roll(w, 1, 1)
+                )
+
+    def block(source, at, links, target, to, k, moved):
+        lane, first = k // half_blocks, k % half_blocks * 16
+        lanes = (
+            pl.ds(pl.multiple_of(lane * 128, 128), 128),
+            pl.ds(pl.multiple_of(plane + lane * 128, 128), 128),
+        )
+        at_rows = [pl.ds(pl.multiple_of(first + 8 * b, 8), 8) for b in range(2)]
+        acc = {}
+
+        def add(b, r, part, value):
+            acc[b, r, part] = value + acc[b, r, part] if (b, r, part) in acc else value
+
+        for way in range(6):
+            direction, back = way // 2, way % 2
+            for c in range(3):
+                fields = []
+                for b in range(2):
+                    if direction == 0:
+                        index = (at + 1 - 2 * back) * 3 + c
+                        fields.append([source[index, at_rows[b], lanes[part]] for part in range(2)])
+                    else:
+                        fields.append([moved[way - 2, c, at_rows[b], lanes[part]] for part in range(2)])
+                for r in range(3):
+                    row = direction * 18 + (54 + c * 6 + r * 2 if back else r * 6 + c * 2)
+                    ur = table[links, row, :, lanes[0]]
+                    ui = table[links, row + 1, :, lanes[0]]
+                    for b, (sr, si) in enumerate(fields):
+                        if back:
+                            add(b, r, 0, ur * sr + ui * si)
+                            add(b, r, 1, ur * si - ui * sr)
+                        else:
+                            add(b, r, 0, ur * sr - ui * si)
+                            add(b, r, 1, ur * si + ui * sr)
+        for (b, r, part), value in acc.items():
+            mid = source[at * 3 + r, at_rows[b], lanes[part]]
+            target[to * 3 + r, at_rows[b], lanes[part]] = mid + KAPPA * (value - 6.0 * mid)
+
+    def sweep(source, offset, target, count):
+        trips = 2 * blocks
+
+        def begin(k, carry):
+            shift(source, 1, k, moved_even)
             return carry
 
-        lax.fori_loop(0, 6, shift, 0)
-
-        def block(lane, carry):
-            lanes = (
-                pl.ds(pl.multiple_of(lane * 128, 128), 128),
-                pl.ds(pl.multiple_of(plane + lane * 128, 128), 128),
-            )
-            acc = {}
-
-            def add(b, r, part, value):
-                acc[b, r, part] = value + acc[b, r, part] if (b, r, part) in acc else value
-
-            for way in range(6):
-                direction, back = way // 2, way % 2
-                for c in range(3):
-                    pair = []
-                    for r in range(3):
-                        row = direction * 18 + (54 + c * 6 + r * 2 if back else r * 6 + c * 2)
-                        pair.append((table[links, row, :, lanes[0]], table[links, row + 1, :, lanes[0]]))
-                    for b in range(blocks):
-                        at_rows = slice(b * 8, b * 8 + 8)
-                        if direction == 0:
-                            index = (at + 1 - 2 * back) * 3 + c
-                            sr = source[index, at_rows, lanes[0]]
-                            si = source[index, at_rows, lanes[1]]
-                        else:
-                            sr = moved[way - 2, c, at_rows, lanes[0]]
-                            si = moved[way - 2, c, at_rows, lanes[1]]
-                        for r, (ur, ui) in enumerate(pair):
-                            if back:
-                                add(b, r, 0, ur * sr + ui * si)
-                                add(b, r, 1, ur * si - ui * sr)
-                            else:
-                                add(b, r, 0, ur * sr - ui * si)
-                                add(b, r, 1, ur * si + ui * sr)
-            for (b, r, part), value in acc.items():
-                at_rows = slice(b * 8, b * 8 + 8)
-                mid = source[at * 3 + r, at_rows, lanes[part]]
-                target[to * 3 + r, at_rows, lanes[part]] = mid + KAPPA * (value - 6.0 * mid)
+        lax.fori_loop(0, trips, begin, 0)
+
+        def one(t, now, later):
+            following = jnp.minimum(t + 1, count - 1) + 1
+
+            def trip(k, carry):
+                shift(source, following, k, later)
+                block(source, t + 1, t + offset, target, t, k, now)
+                return carry
+
+            lax.fori_loop(0, trips, trip, 0)
+
+        def two(h, carry):
+            one(2 * h, moved_even, moved_odd)
+            one(2 * h + 1, moved_odd, moved_even)
             return carry
 
-        lax.fori_loop(0, plane // 128, block, 0)
-
-    def first(t, carry):
-        one_plane(f0, t + 1, t, f1, t)
-        return carry
-
-    lax.fori_loop(0, planes + 2, first, 0)
-
-    def second(t, carry):
-        one_plane(f1, t + 1, t + 1, f0, t)
-        return carry
-
-    lax.fori_loop(0, planes, second, 0)
+        lax.fori_loop(0, count // 2, two, 0)
+        if count % 2:
+            one(count - 1, moved_even, moved_odd)
+
+    sweep(f0, 0, f1, planes + 2)
+    sweep(f1, 1, f0, planes)
 
     def put(k, carry):
         out_ref[k] = f0[k].astype(out_ref.dtype)
@@ -377,6 +390,7 @@
             pltpu.VMEM((planes + 2, 108, 8, plane), jnp.float32),
             pltpu.VMEM(((planes + 4) * 3, rows, 2 * plane), jnp.float32),
             pltpu.VMEM(((planes + 2) * 3, rows, 2 * plane), jnp.float32),
+            pltpu.VMEM((4, 3, rows, 2 * plane), jnp.float32),
             pltpu.VMEM((4, 3, rows, 2 * plane), jnp.float32),
         ],
         compiler_params=pltpu.CompilerParams(vmem_limit_bytes=48 * 2**20),

time: 110 us -> 98.7 us (0.90)
  Pallas kernels: 42.3 us -> 30.8 us
    pallas_call x1, Pallas kernels: 29.2 us -> 17.7 us  [shards_kernels(): pl.pallas_call(functools.partial(smear_kernel, planes, rows), out_shape=j...]
  transfers between devices with their start and end apart: 9 -> 9, of which waited for: 6 -> 6; matrix products, arithmetic and copies ran while one was open for 5% -> 5% of each run, Pallas kernels for 27% -> 18%
where the time goes in v3:
time: 98.7 us; the launch traced here: 98.4 us
  waiting for transfers between devices  41.7 us (42%)
  Pallas kernels  30.8 us (31%)
  starting transfers between devices  13 us (13%)
  local copies, waits for them, and re-layouts  9.26 us (9%)
  other arithmetic  3.34 us (3%)
    ppermute x5, waiting for transfers between devices, from_behind(): lax.ppermute(array, axis, [(i, (i + by) % peers) for i in range(peers)])  24.5 us
    pallas_call x1, Pallas kernels, shards_kernels(): pl.pallas_call(functools.partial(smear_kernel, planes, rows), out_shape=j...  17.7 us
    ppermute x4, waiting for transfers between devices, shards_kernels(): lax.ppermute(blocks[k], ('brick', 'vec', 'sub'), pairs).astype(jnp.float32)  17.2 us
    pallas_call x1, Pallas kernels, shards_kernels(): pl.pallas_call(functools.partial(product_kernel, groups, rows, count, sca...  13.1 us
    ppermute x4, starting transfers between devices, shards_kernels(): lax.ppermute(blocks[k], ('brick', 'vec', 'sub'), pairs).astype(jnp.float32)  6.94 us
    ppermute x5, starting transfers between devices, from_behind(): lax.ppermute(array, axis, [(i, (i + by) % peers) for i in range(peers)])  6.09 us
    reshape x2, local copies, waits for them, and re-layouts, shards_kernels(): vectors.reshape((rows, 3, 2, planes, plane))  3.71 us
  transfers between devices with their start and end apart: 9, of which 6 were waited for; matrix products, arithmetic and copies ran while one was open for 5% of the time, Pallas kernels for 18%

profile of v3, /device:TPU:1, one launch (start us, length us, event | category | flops | bytes accessed | tf_op | source)
XLA Modules:
  0.0 98.4 jit_solution(2390186226981511379)
XLA Ops:
  0.0 2.9 %reshape.170 = f32[32,3,2,4,512]{4,3,2,1,0:T(4,128)S(1)} reshape(f32[32,3,2,2048]{3,2,1,0:T(2,128)} %param.3) | data formatting | bytes 3145728 | tf_op jit(solution)/shard_map/reshape | solution.py:367
  2.9 0.8 copy.9
  3.7 1.4 %reshape.171.x_ref = f32[12,32,1024]{2,1,0:T(8,128)S(1)} reshape(f32[4,3,32,2,512]{4,3,2,1,0:T(2,128)S(1)} %bitcast.12) | data formatting | bytes 3145728 | tf_op jit(solution)/shard_map/reshape | solution.py:368
  5.1 0.1 convert_element_type.32.rest_0_
  5.2 2.1 %collective-permute-start = (bf16[12,32,1024]{2,1,0:T(8,128)(2,1)S(1)}, bf16[12,32,1024]{2,1,0:T(8,128)(2,1)}, u32[]{:S(2)}, u32[]{:S(2)}) collective-permute-start(bf16[12,32,1024]{2,1,0:T(8,128)(2,1)S(1)} %convert_element_type.32.rest_0_), channel_id=1, source_target_pairs={{0,2},{2,0},{1,3},{3,1},{4,6},{6,4},{5,7},{7,5},{8,10},{10,8},{9,1... | collective-permute-start | bytes 2359304 | tf_op jit(solution)/shard_map/ppermute | solution.py:21
  7.3 0.8 fusion.23
  8.1 1.3 %reshape.172.lk_ref = f32[54,2048]{1,0:T(8,128)S(1)} reshape(f32[3,3,3,2,2048]{4,3,2,1,0:T(2,128)} %param.4) | data formatting | bytes 884736 | tf_op jit(solution)/shard_map/reshape | solution.py:370
  9.5 0.8 pad_maximum_fusion
  10.4 1.3 %collective-permute-start.1 = (bf16[8,32,1024]{2,1,0:T(8,128)(2,1)}, bf16[8,32,1024]{2,1,0:T(8,128)(2,1)S(1)}, u32[]{:S(2)}, u32[]{:S(2)}) collective-permute-start(bf16[8,32,1024]{2,1,0:T(8,128)(2,1)} %pad_maximum_fusion), channel_id=1, source_target_pairs={{0,4},{4,8},{8,12},{12,0},{1,5},{5,9},{9,13},{13,1},{2,6},{6,10},{... | collective-permute-start | bytes 1572872 | tf_op jit(solution)/shard_map/ppermute | solution.py:21
  11.7 0.9 pad_maximum_fusion.1
  12.6 2.1 %collective-permute-start.2 = (bf16[8,32,1024]{2,1,0:T(8,128)(2,1)}, bf16[8,32,1024]{2,1,0:T(8,128)(2,1)}, u32[]{:S(2)}, u32[]{:S(2)}) collective-permute-start(bf16[8,32,1024]{2,1,0:T(8,128)(2,1)} %pad_maximum_fusion.1), channel_id=1, source_target_pairs={{0,12},{4,0},{8,4},{12,8},{1,13},{5,1},{9,5},{13,9},{2,14},{6,2},{... | collective-permute-start | bytes 1572872 | tf_op jit(solution)/shard_map/ppermute | solution.py:21
  14.6 10.4 %collective-permute-done.1.lo_ref = bf16[8,32,1024]{2,1,0:T(8,128)(2,1)S(1)} collective-permute-done((bf16[8,32,1024]{2,1,0:T(8,128)(2,1)}, bf16[8,32,1024]{2,1,0:T(8,128)(2,1)S(1)}, u32[]{:S(2)}, u32[]{:S(2)}) %collective-permute-start.1) | collective-permute-done | bytes 524320 | tf_op jit(solution)/shard_map/ppermute | solution.py:21
  25.1 12.6 %collective-permute-done.2.hi_ref = bf16[8,32,1024]{2,1,0:T(8,128)(2,1)} collective-permute-done((bf16[8,32,1024]{2,1,0:T(8,128)(2,1)}, bf16[8,32,1024]{2,1,0:T(8,128)(2,1)}, u32[]{:S(2)}, u32[]{:S(2)}) %collective-permute-start.2) | collective-permute-done | bytes 524320 | tf_op jit(solution)/shard_map/ppermute | solution.py:21
  37.6 17.7 %smear.1.smeared_ref = bf16[12,32,1024]{2,1,0:T(8,128)(2,1)S(1)} custom-call(f32[12,32,1024]{2,1,0:T(8,128)S(1)} %reshape.171.x_ref, bf16[8,32,1024]{2,1,0:T(8,128)(2,1)S(1)} %collective-permute-done.1.lo_ref, bf16[8,32,1024]{2,1,0:T(8,128)(2,1)} %collective-permute-done.2.hi_ref, f32[54,2048]{1,0:T(8,128)S(1)} %reshape.172.lk_ref), custom_call_target="tpu_custom_call" | custom-call | flops 283115520 | bytes 4194304 | tf_op jit(solution)/shard_map/smear/pallas_call | solution.py:383
  55.4 0.0 collective-permute-done.rest_2_
  55.4 0.6 collective-permute-start.3
  56.0 0.1 collective-permute-start.4
  56.1 1.4 %fusion.12 = (f32[4,27,512]{2,1,0:T(8,128)S(1)}, f32[4,27,512]{2,1,0:T(8,128)S(1)}) fusion(s32[4,512]{1,0:T(4,128)S(1)} %get-tuple-element.28, s32[27]{0:T(128)S(1)} %get-tuple-element.26, s32[4,512]{1,0:T(4,128)S(1)} %get-tuple-element.29, s32[27]{0:T(128)S(1)} %get-tuple-element.27, s32[4,512]{1,0:T(4,128)S(1)} %add_select_fusion.6, ...), kind=kLoop, calls=%fused_computation.31 | loop fusion | flops 2488320 | bytes 467268 | tf_op jit(solution)/shard_map/sin | solution.py:356
  57.5 0.4 collective-permute-done.3.rest_1_
  57.9 1.1 %collective-permute-done.4.rest_3_ = bf16[12,32,1024]{2,1,0:T(8,128)(2,1)S(1)} collective-permute-done((bf16[12,32,1024]{2,1,0:T(8,128)(2,1)}, bf16[12,32,1024]{2,1,0:T(8,128)(2,1)S(1)}, u32[]{:S(2)}, u32[]{:S(2)}) %collective-permute-start.4) | collective-permute-done | bytes 786464 | tf_op jit(solution)/shard_map/ppermute | solution.py:21
  59.0 13.1 %product.1 = (bf16[64,864]{1,0:T(8,128)(2,1)S(1)}, bf16[64,864]{1,0:T(8,128)(2,1)S(1)}, bf16[64,864]{1,0:T(8,128)(2,1)S(1)}, bf16[64,864]{1,0:T(8,128)(2,1)S(1)}) custom-call(s32[4]{0:T(128)S(1)} %fusion.17.order_ref, f32[4,27,512]{2,1,0:T(8,128)S(1)} %get-tuple-element.24.cos_ref, f32[4,27,512]{2,1,0:T(8,128)S(1)} %get-tuple-element.23.sin_ref, ...), custom_call_target="tpu_custom_call" | custom-call | flops 5435817984 | bytes 8388608 | tf_op jit(solution)/shard_map/product/pallas_call | solution.py:412
  72.1 2.5 %collective-permute-start.5 = (bf16[64,864]{1,0:T(8,128)(2,1)S(1)}, bf16[64,864]{1,0:T(8,128)(2,1)S(1)}, u32[]{:S(2)}, u32[]{:S(2)}) collective-permute-start(bf16[64,864]{1,0:T(8,128)(2,1)S(1)} %get-tuple-element.15), channel_id=1, source_target_pairs={{0,0},{1,4},{2,8},{3,12},{4,1},{5,5},{6,9},{7,13},{8,2},{9,6},{10,... | collective-permute-start | bytes 331784 | tf_op jit(solution)/shard_map/ppermute | solution.py:440
  74.6 0.1 collective-permute-start.6
  74.6 1.3 %collective-permute-start.7 = (bf16[64,864]{1,0:T(8,128)(2,1)S(1)}, bf16[64,864]{1,0:T(8,128)(2,1)S(1)}, u32[]{:S(2)}, u32[]{:S(2)}) collective-permute-start(bf16[64,864]{1,0:T(8,128)(2,1)S(1)} %get-tuple-element.17), channel_id=1, source_target_pairs={{0,2},{1,6},{2,10},{3,14},{4,3},{5,7},{6,11},{7,15},{8,0},{9,4},{1... | collective-permute-start | bytes 331784 | tf_op jit(solution)/shard_map/ppermute | solution.py:440
  76.0 3.1 %collective-permute-start.8 = (bf16[64,864]{1,0:T(8,128)(2,1)S(1)}, bf16[64,864]{1,0:T(8,128)(2,1)S(1)}, u32[]{:S(2)}, u32[]{:S(2)}) collective-permute-start(bf16[64,864]{1,0:T(8,128)(2,1)S(1)} %get-tuple-element.18), channel_id=1, source_target_pairs={{0,3},{1,7},{2,11},{3,15},{4,0},{5,4},{6,8},{7,12},{8,1},{9,5},{10... | collective-permute-start | bytes 331784 | tf_op jit(solution)/shard_map/ppermute | solution.py:440
  79.1 0.0 collective-permute-done.5
  79.1 0.0 collective-permute-done.6
  79.1 7.0 %collective-permute-done.7 = bf16[64,864]{1,0:T(8,128)(2,1)S(1)} collective-permute-done((bf16[64,864]{1,0:T(8,128)(2,1)S(1)}, bf16[64,864]{1,0:T(8,128)(2,1)S(1)}, u32[]{:S(2)}, u32[]{:S(2)}) %collective-permute-start.7) | collective-permute-done | bytes 110624 | tf_op jit(solution)/shard_map/ppermute | solution.py:440
  86.0 10.3 %collective-permute-done.8 = bf16[64,864]{1,0:T(8,128)(2,1)S(1)} collective-permute-done((bf16[64,864]{1,0:T(8,128)(2,1)S(1)}, bf16[64,864]{1,0:T(8,128)(2,1)S(1)}, u32[]{:S(2)}, u32[]{:S(2)}) %collective-permute-start.8) | collective-permute-done | bytes 110624 | tf_op jit(solution)/shard_map/ppermute | solution.py:440
  96.3 0.1 convert_add_fusion
  96.4 0.4 reshape.175
  96.8 1.6 %copy.7 = f32[32,27,2,32]{3,2,1,0:T(2,128)} copy(f32[32,27,2,32]{3,1,0,2:T(8,128)S(1)} %bitcast.13) | data formatting | bytes 442368 | tf_op jit(solution)/shard_map/transpose | solution.py:442
  (12 shorter events, 0.2 us)
Async XLA Ops:
  5.2 50.2 %collective-permute-start = (bf16[12,32,1024]{2,1,0:T(8,128)(2,1)S(1)}, bf16[12,32,1024]{2,1,0:T(8,128)(2,1)}, u32[]{:S(2)}, u32[]{:S(2)}) collective-permute-start(bf16[12,32,1024]{2,1,0:T(8,128)(2,1)S(1)} %convert_element_type.32.rest_0_), channel_id=1, source_target_pairs={{0,2},{2,0},{1,3},{3,1},{4,6},{6,4},{5,7},{7,5},{8,10},{10,8},{9,1... | collective-permute-start | bytes 2359304 | tf_op jit(solution)/shard_map/ppermute | solution.py:21
  9.5 2.2 %copy-start = (bf16[6,32,1024]{2,1,0:T(8,128)(2,1)S(1)}, bf16[6,32,1024]{2,1,0:T(8,128)(2,1)}, u32[]{:S(2)}) copy-start(bf16[6,32,1024]{2,1,0:T(8,128)(2,1)} %get-tuple-element.19) | copy-start | bytes 1179652
  10.4 14.7 %collective-permute-start.1 = (bf16[8,32,1024]{2,1,0:T(8,128)(2,1)}, bf16[8,32,1024]{2,1,0:T(8,128)(2,1)S(1)}, u32[]{:S(2)}, u32[]{:S(2)}) collective-permute-start(bf16[8,32,1024]{2,1,0:T(8,128)(2,1)} %pad_maximum_fusion), channel_id=1, source_target_pairs={{0,4},{4,8},{8,12},{12,0},{1,5},{5,9},{9,13},{13,1},{2,6},{6,10},{... | collective-permute-start | bytes 1572872 | tf_op jit(solution)/shard_map/ppermute | solution.py:21
  12.6 25.1 %collective-permute-start.2 = (bf16[8,32,1024]{2,1,0:T(8,128)(2,1)}, bf16[8,32,1024]{2,1,0:T(8,128)(2,1)}, u32[]{:S(2)}, u32[]{:S(2)}) collective-permute-start(bf16[8,32,1024]{2,1,0:T(8,128)(2,1)} %pad_maximum_fusion.1), channel_id=1, source_target_pairs={{0,12},{4,0},{8,4},{12,8},{1,13},{5,1},{9,5},{13,9},{2,14},{6,2},{... | collective-permute-start | bytes 1572872 | tf_op jit(solution)/shard_map/ppermute | solution.py:21
  14.6 41.5 %copy-start.1 = (s32[27,3]{0,1:T(4,128)S(1)}, s32[27,3]{0,1:T(4,128)}, u32[]{:S(2)}) copy-start(s32[27,3]{0,1:T(4,128)} %param.5) | copy-start | bytes 976
  55.4 2.5 %collective-permute-start.3 = (bf16[12,32,1024]{2,1,0:T(8,128)(2,1)S(1)}, bf16[12,32,1024]{2,1,0:T(8,128)(2,1)S(1)}, u32[]{:S(2)}, u32[]{:S(2)}) collective-permute-start(bf16[12,32,1024]{2,1,0:T(8,128)(2,1)S(1)} %convert_element_type.32.rest_0_), channel_id=1, source_target_pairs={{0,1},{1,0},{2,3},{3,2},{4,5},{5,4},{6,7},{7,6},{8,9},{9,8},{10,11... | collective-permute-start | bytes 2359304 | tf_op jit(solution)/shard_map/ppermute | solution.py:21
  56.0 3.0 %collective-permute-start.4 = (bf16[12,32,1024]{2,1,0:T(8,128)(2,1)}, bf16[12,32,1024]{2,1,0:T(8,128)(2,1)S(1)}, u32[]{:S(2)}, u32[]{:S(2)}) collective-permute-start(bf16[12,32,1024]{2,1,0:T(8,128)(2,1)} %collective-permute-done.rest_2_), channel_id=1, source_target_pairs={{0,1},{1,0},{2,3},{3,2},{4,5},{5,4},{6,7},{7,6},{8,9},{9,8},{10,11... | collective-permute-start | bytes 2359304 | tf_op jit(solution)/shard_map/ppermute | solution.py:21
  72.1 7.0 %collective-permute-start.5 = (bf16[64,864]{1,0:T(8,128)(2,1)S(1)}, bf16[64,864]{1,0:T(8,128)(2,1)S(1)}, u32[]{:S(2)}, u32[]{:S(2)}) collective-permute-start(bf16[64,864]{1,0:T(8,128)(2,1)S(1)} %get-tuple-element.15), channel_id=1, source_target_pairs={{0,0},{1,4},{2,8},{3,12},{4,1},{5,5},{6,9},{7,13},{8,2},{9,6},{10,... | collective-permute-start | bytes 331784 | tf_op jit(solution)/shard_map/ppermute | solution.py:440
  74.6 4.5 %collective-permute-start.6 = (bf16[64,864]{1,0:T(8,128)(2,1)S(1)}, bf16[64,864]{1,0:T(8,128)(2,1)S(1)}, u32[]{:S(2)}, u32[]{:S(2)}) collective-permute-start(bf16[64,864]{1,0:T(8,128)(2,1)S(1)} %get-tuple-element.16), channel_id=1, source_target_pairs={{0,1},{1,5},{2,9},{3,13},{4,2},{5,6},{6,10},{7,14},{8,3},{9,7},{10... | collective-permute-start | bytes 331784 | tf_op jit(solution)/shard_map/ppermute | solution.py:440
  74.6 11.4 %collective-permute-start.7 = (bf16[64,864]{1,0:T(8,128)(2,1)S(1)}, bf16[64,864]{1,0:T(8,128)(2,1)S(1)}, u32[]{:S(2)}, u32[]{:S(2)}) collective-permute-start(bf16[64,864]{1,0:T(8,128)(2,1)S(1)} %get-tuple-element.17), channel_id=1, source_target_pairs={{0,2},{1,6},{2,10},{3,14},{4,3},{5,7},{6,11},{7,15},{8,0},{9,4},{1... | collective-permute-start | bytes 331784 | tf_op jit(solution)/shard_map/ppermute | solution.py:440
  76.0 20.3 %collective-permute-start.8 = (bf16[64,864]{1,0:T(8,128)(2,1)S(1)}, bf16[64,864]{1,0:T(8,128)(2,1)S(1)}, u32[]{:S(2)}, u32[]{:S(2)}) collective-permute-start(bf16[64,864]{1,0:T(8,128)(2,1)S(1)} %get-tuple-element.18), channel_id=1, source_target_pairs={{0,3},{1,7},{2,11},{3,15},{4,0},{5,4},{6,8},{7,12},{8,1},{9,5},{10... | collective-permute-start | bytes 331784 | tf_op jit(solution)/shard_map/ppermute | solution.py:440
